TPU v7x, 128 devices: a whole 4x4x4 slice. The times are simulated.
128 devices in a mesh: section: 4 (over y), mp: 32 (over x, z, core).
Axes of the slice: x: 4, y: 4, z: 4, core: 2. Of those that a mesh axis runs over, the one named last changes fastest.
Arguments:
- hidden_in: bfloat16 [1, 4, 64, 4096], P(None, 'section'), may hold values from -36 to 36
- attn_gain: bfloat16 [4, 4096], P('section'), may hold values from 0.5 to 2
- w_query: bfloat16 [4, 4096, 4096], P('section', None, 'mp'), may hold values from -0.75 to 0.75
- w_key: bfloat16 [4, 4096, 1024], P('section', None, 'mp'), may hold values from -0.0625 to 0.0625
- w_value: bfloat16 [4, 4096, 1024], P('section', None, 'mp'), may hold values from -0.09375 to 0.09375
- w_out: bfloat16 [4, 4096, 4096], P('section', 'mp'), may hold values from -0.09375 to 0.09375
- ffn_gain: bfloat16 [4, 4096], P('section'), may hold values from 0.5 to 2
- w_gate: bfloat16 [4, 4096, 16384], P('section', None, 'mp'), may hold values from -0.09375 to 0.09375
- w_up: bfloat16 [4, 4096, 16384], P('section', None, 'mp'), may hold values from -0.09375 to 0.09375
- w_down: bfloat16 [4, 16384, 4096], P('section', 'mp'), may hold values from -0.046875 to 0.046875
- ffn_blocks: int32 [4, 4], P(None, 'section'), may hold values from 1 to 112
- heads_on: int32 [4, 4], P(None, 'section'), may hold values from 1 to 32
Outputs:
- hidden_out: bfloat16 [1, 4, 64, 4096], P(None, 'section')
Inputs may be any that keep to these rules, and one draw needn't show every extreme that they name: `ffn_blocks`: hidden units below 128 times the entry are active. `heads_on`: query heads below the entry are active.
All inputs are finite; a program needn't handle non-finite values.
Results may differ from a plain program's by a relative error of at most 0.025.
Values may be sent and summed in bfloat16 or wider, within the bound.
A program may use at most 128 MiB of HBM per device.

v0:
```python
import jax
import jax.numpy as jnp
from jax import lax
from jax.sharding import PartitionSpec as P

HEADS = 32
KV_HEADS = 8
HD = 128
BLOCK = 128
ROPE_BASE = 500000.0
EPSILON = 1e-05


def rows_first(arrays, axis, dims):
    turned = [jnp.moveaxis(a, dim, 0) for a, dim in zip(arrays, dims)]
    widths = [t[0].size for t in turned]
    both = jnp.concatenate([t.reshape(-1, w) for t, w in zip(turned, widths)], axis=1)
    out = lax.all_gather(both, axis, axis=0, tiled=True)
    pieces = jnp.split(out, [sum(widths[:k]) for k in range(1, len(widths))], axis=1)
    return tuple(
        (
            jnp.moveaxis(b.reshape(-1, *t.shape[1:]), 0, dim)
            for b, t, dim in zip(pieces, turned, dims)
        )
    )


def laid_out(pieces, dim):
    pieces = jnp.moveaxis(pieces, 0, dim)
    dims = pieces.shape
    return pieces.reshape(*dims[:dim], dims[dim] * dims[dim + 1], *dims[dim + 2 :])


def sent_to_all(array, axis):
    copies = jnp.broadcast_to(array, (lax.axis_size(axis), *array.shape))
    return lax.all_to_all(copies, axis, split_axis=0, concat_axis=0, tiled=True)


def collect(array, axis, dim):
    return laid_out(sent_to_all(array, axis), dim)


def in_blocks(array, dim, peers):
    dims = array.shape
    pieces = array.reshape(*dims[:dim], peers, dims[dim] // peers, *dims[dim + 1 :])
    return jnp.moveaxis(pieces, dim, 0)


def summed_on_arrival(array, axis, dim):
    peers = lax.axis_size(axis)
    pieces = lax.all_to_all(in_blocks(array, dim, peers), axis, 0, 0, tiled=True)
    return jnp.sum(pieces.astype(jnp.float32), axis=0)


def passed_along(array, axis, by):
    peers = lax.axis_size(axis)
    return lax.ppermute(array, axis, [(i, (i + by) % peers) for i in range(peers)])


def rms_scale(values, gain_row):
    mean_sq = jnp.mean(values * values, axis=-1, keepdims=True)
    return values * lax.rsqrt(mean_sq + EPSILON) * gain_row.astype(jnp.float32)


def rotate(values):
    length = values.shape[0]
    half_dim = values.shape[-1] // 2
    frequency = ROPE_BASE ** (-(jnp.arange(half_dim, dtype=jnp.float32) / half_dim))
    angles = jnp.arange(length, dtype=jnp.float32)[:, None] * frequency[None, :]
    cosine_table = jnp.cos(angles)[:, None, :]
    sine_table = jnp.sin(angles)[:, None, :]
    front_half = values[..., :half_dim].astype(jnp.float32)
    back_half = values[..., half_dim:].astype(jnp.float32)
    return jnp.concatenate(
        [
            front_half * cosine_table - back_half * sine_table,
            front_half * sine_table + back_half * cosine_table,
        ],
        axis=-1,
    )


def attend_local(projected, query_width, key_width, active, first_head):
    length = projected.shape[0]
    heads_here = query_width // HD
    group_size = HEADS // KV_HEADS
    queries = rotate(projected[:, :query_width].reshape(length, heads_here, HD)).astype(
        jnp.bfloat16
    )
    key_local = projected[:, query_width : query_width + key_width].astype(jnp.bfloat16)
    value_local = projected[:, query_width + key_width :].astype(jnp.bfloat16)
    key_whole, value_whole = rows_first((key_local, value_local), "mp", (1, 1))
    key_heads = key_whole.reshape(length, HD, KV_HEADS).transpose(0, 2, 1)
    value_heads = value_whole.reshape(length, HD, KV_HEADS).transpose(0, 2, 1)
    kv_here = max(1, heads_here // group_size)
    repeat_count = heads_here // kv_here
    first_kv = first_head // group_size
    key_pick = lax.dynamic_slice_in_dim(key_heads, first_kv, kv_here, 1)
    value_pick = lax.dynamic_slice_in_dim(value_heads, first_kv, kv_here, 1)
    keys_rot = jnp.repeat(rotate(key_pick).astype(jnp.bfloat16), repeat_count, axis=1)
    values = jnp.repeat(value_pick, repeat_count, axis=1)
    scores = jnp.einsum(
        "qhd,khd->hqk", queries, keys_rot, preferred_element_type=jnp.float32
    ) * HD ** (-0.5)
    causal = jnp.arange(length)[:, None] >= jnp.arange(length)[None, :]
    scores = jnp.where(causal[None], scores, -jnp.inf)
    probabilities = jax.nn.softmax(scores, axis=-1).astype(jnp.bfloat16)
    context = jnp.einsum("hqk,khd->qhd", probabilities, values, preferred_element_type=jnp.float32)
    head_ids = first_head + jnp.arange(heads_here)
    context = jnp.where((head_ids < active)[None, :, None], context, 0.0).astype(jnp.bfloat16)
    return context.reshape(length, query_width)


def per_device(
    hidden_in,
    attn_gain,
    w_query,
    w_key,
    w_value,
    w_out,
    ffn_gain,
    w_gate,
    w_up,
    w_down,
    ffn_blocks,
    heads_on,
):
    section_count = lax.axis_size("section")
    section_index = lax.axis_index("section")
    model_count = lax.axis_size("mp")
    model_index = lax.axis_index("mp")
    micro_total = ffn_blocks.shape[0]
    per_section = hidden_in.shape[0]
    length = hidden_in.shape[2]
    model_width = hidden_in.shape[3]
    local_rows = length // model_count
    units_here = w_gate.shape[2]
    query_width = w_query.shape[2]
    key_width = w_key.shape[2]
    first_head = model_index * (query_width // HD)
    first_unit = model_index * units_here
    joined_qkv = [jnp.concatenate([w_query[0], w_key[0], w_value[0]], axis=1)]
    joined_pair = [jnp.concatenate([w_gate[0], w_up[0]], axis=1)]

    def gated(pre_act, block_count):
        gate_part = pre_act[:, :units_here]
        up_part = pre_act[:, units_here:]
        unit_ids = first_unit + jnp.arange(units_here)
        return jnp.where(
            (unit_ids < BLOCK * block_count)[None, :], jax.nn.silu(gate_part) * up_part, 0.0
        ).astype(jnp.bfloat16)

    def layer_rows(carried, layer_pos, active, block_count):
        residual = carried.astype(jnp.float32)
        normed = rms_scale(residual, attn_gain[layer_pos]).astype(jnp.bfloat16)
        projected = jnp.dot(
            collect(normed, "mp", 0), joined_qkv[layer_pos], preferred_element_type=jnp.float32
        )
        context = attend_local(projected, query_width, key_width, active, first_head)
        attended = residual + summed_on_arrival(
            jnp.dot(context, w_out[layer_pos], preferred_element_type=jnp.float32).astype(
                jnp.bfloat16
            ),
            "mp",
            0,
        )
        normed_ffn = rms_scale(attended, ffn_gain[layer_pos]).astype(jnp.bfloat16)
        hidden = gated(
            jnp.dot(
                collect(normed_ffn, "mp", 0),
                joined_pair[layer_pos],
                preferred_element_type=jnp.float32,
            ),
            block_count,
        )
        return (
            attended
            + summed_on_arrival(
                jnp.dot(hidden, w_down[layer_pos], preferred_element_type=jnp.float32).astype(
                    jnp.bfloat16
                ),
                "mp",
                0,
            )
        ).astype(jnp.bfloat16)

    def section_work(carried, moment, layer_fn):
        micro_index = jnp.clip(moment - section_index, 0, micro_total - 1)
        carried = layer_fn(carried, 0, heads_on[micro_index, 0], ffn_blocks[micro_index, 0])
        return carried

    def tick_step(moment, loop_carry):
        carried, slot_buffer = loop_carry
        cycle_index = moment // section_count
        incoming = lax.dynamic_index_in_dim(
            slot_buffer, jnp.minimum(cycle_index, per_section - 1), 0, keepdims=False
        )
        incoming = jnp.where(moment < micro_total, incoming, jnp.zeros_like(incoming))
        at_head = section_index == 0
        written = lax.dynamic_update_index_in_dim(
            slot_buffer, carried, jnp.maximum(cycle_index - 1, 0), 0
        )
        slot_buffer = jnp.where(at_head & (moment >= section_count), written, slot_buffer)
        carried = jnp.where(at_head, incoming, carried)
        carried = section_work(carried, moment, layer_rows)
        carried = passed_along(carried, "section", 1)
        slot_buffer = passed_along(slot_buffer, "section", -1)
        return (carried, slot_buffer)

    slot_start = hidden_in.reshape(per_section, length, model_width)
    slot_start = lax.dynamic_slice_in_dim(slot_start, model_index * local_rows, local_rows, 1)
    initial = jnp.zeros((local_rows, model_width), jnp.bfloat16)
    finished = lax.fori_loop(0, micro_total + section_count, tick_step, (initial, slot_start))
    result = finished[1]
    result = collect(result, "mp", 1)
    return result.reshape(hidden_in.shape)


def solution(mesh):
    return jax.shard_map(
        per_device,
        mesh=mesh,
        in_specs=(
            P(None, "section", None, None),
            P("section", None),
            P("section", None, "mp"),
            P("section", None, "mp"),
            P("section", None, "mp"),
            P("section", "mp", None),
            P("section", None),
            P("section", None, "mp"),
            P("section", None, "mp"),
            P("section", "mp", None),
            P(None, "section"),
            P(None, "section"),
        ),
        out_specs=P(None, "section", None, None),
        check_vma=False,
    )
```

profile of v0, /device:TPU:1, one launch (start us, length us, event | category | flops | bytes accessed | tf_op | source)
XLA Modules:
  0.0 910.3 jit_solution(10943014542577423044)
XLA Ops:
  4.7 7.9 pad_maximum_fusion.1
  15.2 877.5 %while.21 = (s32[]{:T(128)}, bf16[2,4096]{1,0:T(2,128)(2,1)S(1)}, bf16[1,2,4096]{2,1,0:T(2,128)(2,1)S(1)}, pred[]{:T(512)}, s32[]{:T(128)}, /*index=5*/s32[]{:T(...) while((s32[]{:T(128)}, bf16[2,4096]{1,0:T(2,128)(2,1)S(1)}, ...), condition=%wide.region_7.8_spmd, body=%wide.region_0.7_spmd.sunk | while | flops 977384448 | bytes 49139016 | solution.py:213
  16.8 9.4 %all-to-all-start = ((bf16[32,2,4096]{2,1,0:T(2,128)(2,1)}), bf16[32,2,4096]{2,1,0:T(2,128)(2,1)S(1)}, u32[]{:S(2)}, u32[]{:S(2)}) async-start(bf16[32,2,4096]{2,1,0:T(2,128)(2,1)} %broadcast_in_dim.182), calls=%async_computation | async-start | bytes 1048576 | tf_op jit(solution)/shard_map/while/body/eval_jaxpr/all_to_all | solution.py:36
  27.5 10.3 %all-to-all-done = bf16[32,2,4096]{2,1,0:T(2,128)(2,1)S(1)} async-done(((bf16[32,2,4096]{2,1,0:T(2,128)(2,1)}), bf16[32,2,4096]{2,1,0:T(2,128)(2,1)S(1)}, u32[]{:S(2)}, u32[]{:S(2)}) %all-to-all-start) | async-done | bytes 524320 | tf_op jit(solution)/shard_map/while/body/eval_jaxpr/all_to_all | solution.py:36
  40.6 22.9 %all_gather.11 = bf16[1024,128]{1,0:T(8,128)(2,1)S(1)} all-gather(bf16[32,128]{1,0:T(8,128)(2,1)S(1)} %pad_maximum_fusion.4), channel_id=1, replica_groups=mesh['section'=4,'mp'=32] {'mp'}, dimensions={0}, use_global_device_ids=true | all-gather | bytes 270336 | tf_op jit(solution)/shard_map/while/body/eval_jaxpr/all_gather | solution.py:18
  71.9 11.6 %all-to-all-done.1 = bf16[32,2,4096]{2,1,0:T(2,128)(2,1)S(1)} async-done(((bf16[32,2,4096]{2,1,0:T(2,128)(2,1)}), bf16[32,2,4096]{2,1,0:T(2,128)(2,1)S(1)}, u32[]{:S(2)}, u32[]{:S(2)}) %all-to-all-start.1) | async-done | bytes 524320 | tf_op jit(solution)/shard_map/while/body/eval_jaxpr/all_to_all | solution.py:51
  91.1 10.0 %all-to-all-done.2 = bf16[32,2,4096]{2,1,0:T(2,128)(2,1)} async-done(((bf16[32,2,4096]{2,1,0:T(2,128)(2,1)}), bf16[32,2,4096]{2,1,0:T(2,128)(2,1)}, u32[]{:S(2)}, u32[]{:S(2)}) %all-to-all-start.2) | async-done | bytes 524320 | tf_op jit(solution)/shard_map/while/body/eval_jaxpr/all_to_all | solution.py:36
  102.4 5.1 fusion.82
  116.0 8.7 all-to-all-done.3
  136.6 10.3 %all-to-all-done = bf16[32,2,4096]{2,1,0:T(2,128)(2,1)S(1)} async-done(((bf16[32,2,4096]{2,1,0:T(2,128)(2,1)}), bf16[32,2,4096]{2,1,0:T(2,128)(2,1)S(1)}, u32[]{:S(2)}, u32[]{:S(2)}) %all-to-all-start) | async-done | bytes 524320 | tf_op jit(solution)/shard_map/while/body/eval_jaxpr/all_to_all | solution.py:36
  149.7 22.9 %all_gather.11 = bf16[1024,128]{1,0:T(8,128)(2,1)S(1)} all-gather(bf16[32,128]{1,0:T(8,128)(2,1)S(1)} %pad_maximum_fusion.4), channel_id=1, replica_groups=mesh['section'=4,'mp'=32] {'mp'}, dimensions={0}, use_global_device_ids=true | all-gather | bytes 270336 | tf_op jit(solution)/shard_map/while/body/eval_jaxpr/all_gather | solution.py:18
  181.0 11.6 %all-to-all-done.1 = bf16[32,2,4096]{2,1,0:T(2,128)(2,1)S(1)} async-done(((bf16[32,2,4096]{2,1,0:T(2,128)(2,1)}), bf16[32,2,4096]{2,1,0:T(2,128)(2,1)S(1)}, u32[]{:S(2)}, u32[]{:S(2)}) %all-to-all-start.1) | async-done | bytes 524320 | tf_op jit(solution)/shard_map/while/body/eval_jaxpr/all_to_all | solution.py:51
  200.2 10.0 %all-to-all-done.2 = bf16[32,2,4096]{2,1,0:T(2,128)(2,1)} async-done(((bf16[32,2,4096]{2,1,0:T(2,128)(2,1)}), bf16[32,2,4096]{2,1,0:T(2,128)(2,1)}, u32[]{:S(2)}, u32[]{:S(2)}) %all-to-all-start.2) | async-done | bytes 524320 | tf_op jit(solution)/shard_map/while/body/eval_jaxpr/all_to_all | solution.py:36
  211.5 5.1 fusion.82
  223.9 9.9 %all-to-all-done.3 = bf16[32,2,4096]{2,1,0:T(2,128)(2,1)S(1)} async-done(((bf16[32,2,4096]{2,1,0:T(2,128)(2,1)}), bf16[32,2,4096]{2,1,0:T(2,128)(2,1)S(1)}, u32[]{:S(2)}, u32[]{:S(2)}) %all-to-all-start.3) | async-done | bytes 524320 | tf_op jit(solution)/shard_map/while/body/eval_jaxpr/all_to_all | solution.py:51
  245.7 10.3 %all-to-all-done = bf16[32,2,4096]{2,1,0:T(2,128)(2,1)S(1)} async-done(((bf16[32,2,4096]{2,1,0:T(2,128)(2,1)}), bf16[32,2,4096]{2,1,0:T(2,128)(2,1)S(1)}, u32[]{:S(2)}, u32[]{:S(2)}) %all-to-all-start) | async-done | bytes 524320 | tf_op jit(solution)/shard_map/while/body/eval_jaxpr/all_to_all | solution.py:36
  258.8 22.9 %all_gather.11 = bf16[1024,128]{1,0:T(8,128)(2,1)S(1)} all-gather(bf16[32,128]{1,0:T(8,128)(2,1)S(1)} %pad_maximum_fusion.4), channel_id=1, replica_groups=mesh['section'=4,'mp'=32] {'mp'}, dimensions={0}, use_global_device_ids=true | all-gather | bytes 270336 | tf_op jit(solution)/shard_map/while/body/eval_jaxpr/all_gather | solution.py:18
  290.1 11.6 %all-to-all-done.1 = bf16[32,2,4096]{2,1,0:T(2,128)(2,1)S(1)} async-done(((bf16[32,2,4096]{2,1,0:T(2,128)(2,1)}), bf16[32,2,4096]{2,1,0:T(2,128)(2,1)S(1)}, u32[]{:S(2)}, u32[]{:S(2)}) %all-to-all-start.1) | async-done | bytes 524320 | tf_op jit(solution)/shard_map/while/body/eval_jaxpr/all_to_all | solution.py:51
  309.3 10.0 %all-to-all-done.2 = bf16[32,2,4096]{2,1,0:T(2,128)(2,1)} async-done(((bf16[32,2,4096]{2,1,0:T(2,128)(2,1)}), bf16[32,2,4096]{2,1,0:T(2,128)(2,1)}, u32[]{:S(2)}, u32[]{:S(2)}) %all-to-all-start.2) | async-done | bytes 524320 | tf_op jit(solution)/shard_map/while/body/eval_jaxpr/all_to_all | solution.py:36
  320.6 5.1 fusion.82
  331.8 11.1 %all-to-all-done.3 = bf16[32,2,4096]{2,1,0:T(2,128)(2,1)S(1)} async-done(((bf16[32,2,4096]{2,1,0:T(2,128)(2,1)}), bf16[32,2,4096]{2,1,0:T(2,128)(2,1)S(1)}, u32[]{:S(2)}, u32[]{:S(2)}) %all-to-all-start.3) | async-done | bytes 524320 | tf_op jit(solution)/shard_map/while/body/eval_jaxpr/all_to_all | solution.py:51
  354.8 10.3 %all-to-all-done = bf16[32,2,4096]{2,1,0:T(2,128)(2,1)S(1)} async-done(((bf16[32,2,4096]{2,1,0:T(2,128)(2,1)}), bf16[32,2,4096]{2,1,0:T(2,128)(2,1)S(1)}, u32[]{:S(2)}, u32[]{:S(2)}) %all-to-all-start) | async-done | bytes 524320 | tf_op jit(solution)/shard_map/while/body/eval_jaxpr/all_to_all | solution.py:36
  367.9 22.9 %all_gather.11 = bf16[1024,128]{1,0:T(8,128)(2,1)S(1)} all-gather(bf16[32,128]{1,0:T(8,128)(2,1)S(1)} %pad_maximum_fusion.4), channel_id=1, replica_groups=mesh['section'=4,'mp'=32] {'mp'}, dimensions={0}, use_global_device_ids=true | all-gather | bytes 270336 | tf_op jit(solution)/shard_map/while/body/eval_jaxpr/all_gather | solution.py:18
  399.2 11.6 %all-to-all-done.1 = bf16[32,2,4096]{2,1,0:T(2,128)(2,1)S(1)} async-done(((bf16[32,2,4096]{2,1,0:T(2,128)(2,1)}), bf16[32,2,4096]{2,1,0:T(2,128)(2,1)S(1)}, u32[]{:S(2)}, u32[]{:S(2)}) %all-to-all-start.1) | async-done | bytes 524320 | tf_op jit(solution)/shard_map/while/body/eval_jaxpr/all_to_all | solution.py:51
  418.4 10.0 %all-to-all-done.2 = bf16[32,2,4096]{2,1,0:T(2,128)(2,1)} async-done(((bf16[32,2,4096]{2,1,0:T(2,128)(2,1)}), bf16[32,2,4096]{2,1,0:T(2,128)(2,1)}, u32[]{:S(2)}, u32[]{:S(2)}) %all-to-all-start.2) | async-done | bytes 524320 | tf_op jit(solution)/shard_map/while/body/eval_jaxpr/all_to_all | solution.py:36
  440.6 11.4 %all-to-all-done.3 = bf16[32,2,4096]{2,1,0:T(2,128)(2,1)S(1)} async-done(((bf16[32,2,4096]{2,1,0:T(2,128)(2,1)}), bf16[32,2,4096]{2,1,0:T(2,128)(2,1)S(1)}, u32[]{:S(2)}, u32[]{:S(2)}) %all-to-all-start.3) | async-done | bytes 524320 | tf_op jit(solution)/shard_map/while/body/eval_jaxpr/all_to_all | solution.py:51
  463.9 10.3 %all-to-all-done = bf16[32,2,4096]{2,1,0:T(2,128)(2,1)S(1)} async-done(((bf16[32,2,4096]{2,1,0:T(2,128)(2,1)}), bf16[32,2,4096]{2,1,0:T(2,128)(2,1)S(1)}, u32[]{:S(2)}, u32[]{:S(2)}) %all-to-all-start) | async-done | bytes 524320 | tf_op jit(solution)/shard_map/while/body/eval_jaxpr/all_to_all | solution.py:36
  477.0 22.9 %all_gather.11 = bf16[1024,128]{1,0:T(8,128)(2,1)S(1)} all-gather(bf16[32,128]{1,0:T(8,128)(2,1)S(1)} %pad_maximum_fusion.4), channel_id=1, replica_groups=mesh['section'=4,'mp'=32] {'mp'}, dimensions={0}, use_global_device_ids=true | all-gather | bytes 270336 | tf_op jit(solution)/shard_map/while/body/eval_jaxpr/all_gather | solution.py:18
  508.3 11.6 %all-to-all-done.1 = bf16[32,2,4096]{2,1,0:T(2,128)(2,1)S(1)} async-done(((bf16[32,2,4096]{2,1,0:T(2,128)(2,1)}), bf16[32,2,4096]{2,1,0:T(2,128)(2,1)S(1)}, u32[]{:S(2)}, u32[]{:S(2)}) %all-to-all-start.1) | async-done | bytes 524320 | tf_op jit(solution)/shard_map/while/body/eval_jaxpr/all_to_all | solution.py:51
  527.5 10.0 %all-to-all-done.2 = bf16[32,2,4096]{2,1,0:T(2,128)(2,1)} async-done(((bf16[32,2,4096]{2,1,0:T(2,128)(2,1)}), bf16[32,2,4096]{2,1,0:T(2,128)(2,1)}, u32[]{:S(2)}, u32[]{:S(2)}) %all-to-all-start.2) | async-done | bytes 524320 | tf_op jit(solution)/shard_map/while/body/eval_jaxpr/all_to_all | solution.py:36
  549.7 11.4 %all-to-all-done.3 = bf16[32,2,4096]{2,1,0:T(2,128)(2,1)S(1)} async-done(((bf16[32,2,4096]{2,1,0:T(2,128)(2,1)}), bf16[32,2,4096]{2,1,0:T(2,128)(2,1)S(1)}, u32[]{:S(2)}, u32[]{:S(2)}) %all-to-all-start.3) | async-done | bytes 524320 | tf_op jit(solution)/shard_map/while/body/eval_jaxpr/all_to_all | solution.py:51
  573.0 10.3 %all-to-all-done = bf16[32,2,4096]{2,1,0:T(2,128)(2,1)S(1)} async-done(((bf16[32,2,4096]{2,1,0:T(2,128)(2,1)}), bf16[32,2,4096]{2,1,0:T(2,128)(2,1)S(1)}, u32[]{:S(2)}, u32[]{:S(2)}) %all-to-all-start) | async-done | bytes 524320 | tf_op jit(solution)/shard_map/while/body/eval_jaxpr/all_to_all | solution.py:36
  586.1 22.9 %all_gather.11 = bf16[1024,128]{1,0:T(8,128)(2,1)S(1)} all-gather(bf16[32,128]{1,0:T(8,128)(2,1)S(1)} %pad_maximum_fusion.4), channel_id=1, replica_groups=mesh['section'=4,'mp'=32] {'mp'}, dimensions={0}, use_global_device_ids=true | all-gather | bytes 270336 | tf_op jit(solution)/shard_map/while/body/eval_jaxpr/all_gather | solution.py:18
  617.4 11.6 %all-to-all-done.1 = bf16[32,2,4096]{2,1,0:T(2,128)(2,1)S(1)} async-done(((bf16[32,2,4096]{2,1,0:T(2,128)(2,1)}), bf16[32,2,4096]{2,1,0:T(2,128)(2,1)S(1)}, u32[]{:S(2)}, u32[]{:S(2)}) %all-to-all-start.1) | async-done | bytes 524320 | tf_op jit(solution)/shard_map/while/body/eval_jaxpr/all_to_all | solution.py:51
  636.6 10.0 %all-to-all-done.2 = bf16[32,2,4096]{2,1,0:T(2,128)(2,1)} async-done(((bf16[32,2,4096]{2,1,0:T(2,128)(2,1)}), bf16[32,2,4096]{2,1,0:T(2,128)(2,1)}, u32[]{:S(2)}, u32[]{:S(2)}) %all-to-all-start.2) | async-done | bytes 524320 | tf_op jit(solution)/shard_map/while/body/eval_jaxpr/all_to_all | solution.py:36
  658.8 11.4 %all-to-all-done.3 = bf16[32,2,4096]{2,1,0:T(2,128)(2,1)S(1)} async-done(((bf16[32,2,4096]{2,1,0:T(2,128)(2,1)}), bf16[32,2,4096]{2,1,0:T(2,128)(2,1)S(1)}, u32[]{:S(2)}, u32[]{:S(2)}) %all-to-all-start.3) | async-done | bytes 524320 | tf_op jit(solution)/shard_map/while/body/eval_jaxpr/all_to_all | solution.py:51
  682.1 10.3 %all-to-all-done = bf16[32,2,4096]{2,1,0:T(2,128)(2,1)S(1)} async-done(((bf16[32,2,4096]{2,1,0:T(2,128)(2,1)}), bf16[32,2,4096]{2,1,0:T(2,128)(2,1)S(1)}, u32[]{:S(2)}, u32[]{:S(2)}) %all-to-all-start) | async-done | bytes 524320 | tf_op jit(solution)/shard_map/while/body/eval_jaxpr/all_to_all | solution.py:36
  695.2 22.9 %all_gather.11 = bf16[1024,128]{1,0:T(8,128)(2,1)S(1)} all-gather(bf16[32,128]{1,0:T(8,128)(2,1)S(1)} %pad_maximum_fusion.4), channel_id=1, replica_groups=mesh['section'=4,'mp'=32] {'mp'}, dimensions={0}, use_global_device_ids=true | all-gather | bytes 270336 | tf_op jit(solution)/shard_map/while/body/eval_jaxpr/all_gather | solution.py:18
  726.5 11.6 %all-to-all-done.1 = bf16[32,2,4096]{2,1,0:T(2,128)(2,1)S(1)} async-done(((bf16[32,2,4096]{2,1,0:T(2,128)(2,1)}), bf16[32,2,4096]{2,1,0:T(2,128)(2,1)S(1)}, u32[]{:S(2)}, u32[]{:S(2)}) %all-to-all-start.1) | async-done | bytes 524320 | tf_op jit(solution)/shard_map/while/body/eval_jaxpr/all_to_all | solution.py:51
  745.7 10.0 %all-to-all-done.2 = bf16[32,2,4096]{2,1,0:T(2,128)(2,1)} async-done(((bf16[32,2,4096]{2,1,0:T(2,128)(2,1)}), bf16[32,2,4096]{2,1,0:T(2,128)(2,1)}, u32[]{:S(2)}, u32[]{:S(2)}) %all-to-all-start.2) | async-done | bytes 524320 | tf_op jit(solution)/shard_map/while/body/eval_jaxpr/all_to_all | solution.py:36
  767.9 11.4 %all-to-all-done.3 = bf16[32,2,4096]{2,1,0:T(2,128)(2,1)S(1)} async-done(((bf16[32,2,4096]{2,1,0:T(2,128)(2,1)}), bf16[32,2,4096]{2,1,0:T(2,128)(2,1)S(1)}, u32[]{:S(2)}, u32[]{:S(2)}) %all-to-all-start.3) | async-done | bytes 524320 | tf_op jit(solution)/shard_map/while/body/eval_jaxpr/all_to_all | solution.py:51
  791.2 10.3 %all-to-all-done = bf16[32,2,4096]{2,1,0:T(2,128)(2,1)S(1)} async-done(((bf16[32,2,4096]{2,1,0:T(2,128)(2,1)}), bf16[32,2,4096]{2,1,0:T(2,128)(2,1)S(1)}, u32[]{:S(2)}, u32[]{:S(2)}) %all-to-all-start) | async-done | bytes 524320 | tf_op jit(solution)/shard_map/while/body/eval_jaxpr/all_to_all | solution.py:36
  804.3 22.9 %all_gather.11 = bf16[1024,128]{1,0:T(8,128)(2,1)S(1)} all-gather(bf16[32,128]{1,0:T(8,128)(2,1)S(1)} %pad_maximum_fusion.4), channel_id=1, replica_groups=mesh['section'=4,'mp'=32] {'mp'}, dimensions={0}, use_global_device_ids=true | all-gather | bytes 270336 | tf_op jit(solution)/shard_map/while/body/eval_jaxpr/all_gather | solution.py:18
  835.6 11.6 %all-to-all-done.1 = bf16[32,2,4096]{2,1,0:T(2,128)(2,1)S(1)} async-done(((bf16[32,2,4096]{2,1,0:T(2,128)(2,1)}), bf16[32,2,4096]{2,1,0:T(2,128)(2,1)S(1)}, u32[]{:S(2)}, u32[]{:S(2)}) %all-to-all-start.1) | async-done | bytes 524320 | tf_op jit(solution)/shard_map/while/body/eval_jaxpr/all_to_all | solution.py:51
  854.8 10.0 %all-to-all-done.2 = bf16[32,2,4096]{2,1,0:T(2,128)(2,1)} async-done(((bf16[32,2,4096]{2,1,0:T(2,128)(2,1)}), bf16[32,2,4096]{2,1,0:T(2,128)(2,1)}, u32[]{:S(2)}, u32[]{:S(2)}) %all-to-all-start.2) | async-done | bytes 524320 | tf_op jit(solution)/shard_map/while/body/eval_jaxpr/all_to_all | solution.py:36
  866.1 5.1 fusion.82
  877.0 11.4 %all-to-all-done.3 = bf16[32,2,4096]{2,1,0:T(2,128)(2,1)S(1)} async-done(((bf16[32,2,4096]{2,1,0:T(2,128)(2,1)}), bf16[32,2,4096]{2,1,0:T(2,128)(2,1)S(1)}, u32[]{:S(2)}, u32[]{:S(2)}) %all-to-all-start.3) | async-done | bytes 524320 | tf_op jit(solution)/shard_map/while/body/eval_jaxpr/all_to_all | solution.py:51
  893.2 16.2 %all_to_all.57 = bf16[32,1,2,4096]{3,2,1,0:T(2,128)(2,1)S(1)} all-to-all(bf16[32,1,2,4096]{3,2,1,0:T(2,128)(2,1)S(1)} %broadcast_in_dim.154), channel_id=1, replica_groups=mesh['section'=4,'mp'=32] {'mp'}, dimensions={0} | all-to-all | bytes 1048576 | tf_op jit(solution)/shard_map/all_to_all | solution.py:36
  (396 shorter events, 324.1 us)
Async XLA Ops:
  16.8 21.0 %all-to-all-start = ((bf16[32,2,4096]{2,1,0:T(2,128)(2,1)}), bf16[32,2,4096]{2,1,0:T(2,128)(2,1)S(1)}, u32[]{:S(2)}, u32[]{:S(2)}) async-start(bf16[32,2,4096]{2,1,0:T(2,128)(2,1)} %broadcast_in_dim.182), calls=%async_computation | async-start | bytes 1048576 | tf_op jit(solution)/shard_map/while/body/eval_jaxpr/all_to_all | solution.py:36
  67.4 16.1 %all-to-all-start.1 = ((bf16[32,2,4096]{2,1,0:T(2,128)(2,1)}), bf16[32,2,4096]{2,1,0:T(2,128)(2,1)S(1)}, u32[]{:S(2)}, u32[]{:S(2)}) async-start(bf16[32,2,4096]{2,1,0:T(2,128)(2,1)} %reshape.303), calls=%async_computation.1 | async-start | bytes 1048576 | tf_op jit(solution)/shard_map/while/body/eval_jaxpr/all_to_all | solution.py:51
  85.4 15.7 %all-to-all-start.2 = ((bf16[32,2,4096]{2,1,0:T(2,128)(2,1)}), bf16[32,2,4096]{2,1,0:T(2,128)(2,1)}, u32[]{:S(2)}, u32[]{:S(2)}) async-start(bf16[32,2,4096]{2,1,0:T(2,128)(2,1)} %broadcast_in_dim.183), calls=%async_computation.2 | async-start | bytes 1048576 | tf_op jit(solution)/shard_map/while/body/eval_jaxpr/all_to_all | solution.py:36
  109.4 15.2 %all-to-all-start.3 = ((bf16[32,2,4096]{2,1,0:T(2,128)(2,1)}), bf16[32,2,4096]{2,1,0:T(2,128)(2,1)S(1)}, u32[]{:S(2)}, u32[]{:S(2)}) async-start(bf16[32,2,4096]{2,1,0:T(2,128)(2,1)} %reshape.305), calls=%async_computation.3 | async-start | bytes 1048576 | tf_op jit(solution)/shard_map/while/body/eval_jaxpr/all_to_all | solution.py:51
  113.2 13.3 %collective-permute-start.1 = (bf16[1,2,4096]{2,1,0:T(2,128)(2,1)S(1)}, bf16[1,2,4096]{2,1,0:T(2,128)(2,1)S(1)}, u32[]{:S(2)}, u32[]{:S(2)}) collective-permute-start(bf16[1,2,4096]{2,1,0:T(2,128)(2,1)S(1)} %broadcast_select_fusion.5), channel_id=1, source_target_pairs={{0,96},{32,0},{64,32},{96,64},{1,97},{33,1},{65,33},{97,65},{2,98}... | collective-permute-start | bytes 49160 | tf_op jit(solution)/shard_map/while/body/eval_jaxpr/ppermute | solution.py:57
  125.1 4.3 collective-permute-start
  130.9 16.0 %all-to-all-start = ((bf16[32,2,4096]{2,1,0:T(2,128)(2,1)}), bf16[32,2,4096]{2,1,0:T(2,128)(2,1)S(1)}, u32[]{:S(2)}, u32[]{:S(2)}) async-start(bf16[32,2,4096]{2,1,0:T(2,128)(2,1)} %broadcast_in_dim.182), calls=%async_computation | async-start | bytes 1048576 | tf_op jit(solution)/shard_map/while/body/eval_jaxpr/all_to_all | solution.py:36
  176.5 16.1 %all-to-all-start.1 = ((bf16[32,2,4096]{2,1,0:T(2,128)(2,1)}), bf16[32,2,4096]{2,1,0:T(2,128)(2,1)S(1)}, u32[]{:S(2)}, u32[]{:S(2)}) async-start(bf16[32,2,4096]{2,1,0:T(2,128)(2,1)} %reshape.303), calls=%async_computation.1 | async-start | bytes 1048576 | tf_op jit(solution)/shard_map/while/body/eval_jaxpr/all_to_all | solution.py:51
  194.5 15.7 %all-to-all-start.2 = ((bf16[32,2,4096]{2,1,0:T(2,128)(2,1)}), bf16[32,2,4096]{2,1,0:T(2,128)(2,1)}, u32[]{:S(2)}, u32[]{:S(2)}) async-start(bf16[32,2,4096]{2,1,0:T(2,128)(2,1)} %broadcast_in_dim.183), calls=%async_computation.2 | async-start | bytes 1048576 | tf_op jit(solution)/shard_map/while/body/eval_jaxpr/all_to_all | solution.py:36
  218.6 15.2 %all-to-all-start.3 = ((bf16[32,2,4096]{2,1,0:T(2,128)(2,1)}), bf16[32,2,4096]{2,1,0:T(2,128)(2,1)S(1)}, u32[]{:S(2)}, u32[]{:S(2)}) async-start(bf16[32,2,4096]{2,1,0:T(2,128)(2,1)} %reshape.305), calls=%async_computation.3 | async-start | bytes 1048576 | tf_op jit(solution)/shard_map/while/body/eval_jaxpr/all_to_all | solution.py:51
  222.3 12.1 %collective-permute-start.1 = (bf16[1,2,4096]{2,1,0:T(2,128)(2,1)S(1)}, bf16[1,2,4096]{2,1,0:T(2,128)(2,1)S(1)}, u32[]{:S(2)}, u32[]{:S(2)}) collective-permute-start(bf16[1,2,4096]{2,1,0:T(2,128)(2,1)S(1)} %broadcast_select_fusion.5), channel_id=1, source_target_pairs={{0,96},{32,0},{64,32},{96,64},{1,97},{33,1},{65,33},{97,65},{2,98}... | collective-permute-start | bytes 49160 | tf_op jit(solution)/shard_map/while/body/eval_jaxpr/ppermute | solution.py:57
  234.2 3.9 collective-permute-start
  239.6 16.4 %all-to-all-start = ((bf16[32,2,4096]{2,1,0:T(2,128)(2,1)}), bf16[32,2,4096]{2,1,0:T(2,128)(2,1)S(1)}, u32[]{:S(2)}, u32[]{:S(2)}) async-start(bf16[32,2,4096]{2,1,0:T(2,128)(2,1)} %broadcast_in_dim.182), calls=%async_computation | async-start | bytes 1048576 | tf_op jit(solution)/shard_map/while/body/eval_jaxpr/all_to_all | solution.py:36
  285.6 16.1 %all-to-all-start.1 = ((bf16[32,2,4096]{2,1,0:T(2,128)(2,1)}), bf16[32,2,4096]{2,1,0:T(2,128)(2,1)S(1)}, u32[]{:S(2)}, u32[]{:S(2)}) async-start(bf16[32,2,4096]{2,1,0:T(2,128)(2,1)} %reshape.303), calls=%async_computation.1 | async-start | bytes 1048576 | tf_op jit(solution)/shard_map/while/body/eval_jaxpr/all_to_all | solution.py:51
  303.6 15.7 %all-to-all-start.2 = ((bf16[32,2,4096]{2,1,0:T(2,128)(2,1)}), bf16[32,2,4096]{2,1,0:T(2,128)(2,1)}, u32[]{:S(2)}, u32[]{:S(2)}) async-start(bf16[32,2,4096]{2,1,0:T(2,128)(2,1)} %broadcast_in_dim.183), calls=%async_computation.2 | async-start | bytes 1048576 | tf_op jit(solution)/shard_map/while/body/eval_jaxpr/all_to_all | solution.py:36
  327.7 15.2 %all-to-all-start.3 = ((bf16[32,2,4096]{2,1,0:T(2,128)(2,1)}), bf16[32,2,4096]{2,1,0:T(2,128)(2,1)S(1)}, u32[]{:S(2)}, u32[]{:S(2)}) async-start(bf16[32,2,4096]{2,1,0:T(2,128)(2,1)} %reshape.305), calls=%async_computation.3 | async-start | bytes 1048576 | tf_op jit(solution)/shard_map/while/body/eval_jaxpr/all_to_all | solution.py:51
  331.4 12.0 %collective-permute-start.1 = (bf16[1,2,4096]{2,1,0:T(2,128)(2,1)S(1)}, bf16[1,2,4096]{2,1,0:T(2,128)(2,1)S(1)}, u32[]{:S(2)}, u32[]{:S(2)}) collective-permute-start(bf16[1,2,4096]{2,1,0:T(2,128)(2,1)S(1)} %broadcast_select_fusion.5), channel_id=1, source_target_pairs={{0,96},{32,0},{64,32},{96,64},{1,97},{33,1},{65,33},{97,65},{2,98}... | collective-permute-start | bytes 49160 | tf_op jit(solution)/shard_map/while/body/eval_jaxpr/ppermute | solution.py:57
  343.3 3.9 collective-permute-start
  348.7 16.4 %all-to-all-start = ((bf16[32,2,4096]{2,1,0:T(2,128)(2,1)}), bf16[32,2,4096]{2,1,0:T(2,128)(2,1)S(1)}, u32[]{:S(2)}, u32[]{:S(2)}) async-start(bf16[32,2,4096]{2,1,0:T(2,128)(2,1)} %broadcast_in_dim.182), calls=%async_computation | async-start | bytes 1048576 | tf_op jit(solution)/shard_map/while/body/eval_jaxpr/all_to_all | solution.py:36
  394.7 16.1 %all-to-all-start.1 = ((bf16[32,2,4096]{2,1,0:T(2,128)(2,1)}), bf16[32,2,4096]{2,1,0:T(2,128)(2,1)S(1)}, u32[]{:S(2)}, u32[]{:S(2)}) async-start(bf16[32,2,4096]{2,1,0:T(2,128)(2,1)} %reshape.303), calls=%async_computation.1 | async-start | bytes 1048576 | tf_op jit(solution)/shard_map/while/body/eval_jaxpr/all_to_all | solution.py:51
  412.7 15.7 %all-to-all-start.2 = ((bf16[32,2,4096]{2,1,0:T(2,128)(2,1)}), bf16[32,2,4096]{2,1,0:T(2,128)(2,1)}, u32[]{:S(2)}, u32[]{:S(2)}) async-start(bf16[32,2,4096]{2,1,0:T(2,128)(2,1)} %broadcast_in_dim.183), calls=%async_computation.2 | async-start | bytes 1048576 | tf_op jit(solution)/shard_map/while/body/eval_jaxpr/all_to_all | solution.py:36
  436.8 15.2 %all-to-all-start.3 = ((bf16[32,2,4096]{2,1,0:T(2,128)(2,1)}), bf16[32,2,4096]{2,1,0:T(2,128)(2,1)S(1)}, u32[]{:S(2)}, u32[]{:S(2)}) async-start(bf16[32,2,4096]{2,1,0:T(2,128)(2,1)} %reshape.305), calls=%async_computation.3 | async-start | bytes 1048576 | tf_op jit(solution)/shard_map/while/body/eval_jaxpr/all_to_all | solution.py:51
  440.5 12.0 %collective-permute-start.1 = (bf16[1,2,4096]{2,1,0:T(2,128)(2,1)S(1)}, bf16[1,2,4096]{2,1,0:T(2,128)(2,1)S(1)}, u32[]{:S(2)}, u32[]{:S(2)}) collective-permute-start(bf16[1,2,4096]{2,1,0:T(2,128)(2,1)S(1)} %broadcast_select_fusion.5), channel_id=1, source_target_pairs={{0,96},{32,0},{64,32},{96,64},{1,97},{33,1},{65,33},{97,65},{2,98}... | collective-permute-start | bytes 49160 | tf_op jit(solution)/shard_map/while/body/eval_jaxpr/ppermute | solution.py:57
  452.4 3.9 collective-permute-start
  457.8 16.4 %all-to-all-start = ((bf16[32,2,4096]{2,1,0:T(2,128)(2,1)}), bf16[32,2,4096]{2,1,0:T(2,128)(2,1)S(1)}, u32[]{:S(2)}, u32[]{:S(2)}) async-start(bf16[32,2,4096]{2,1,0:T(2,128)(2,1)} %broadcast_in_dim.182), calls=%async_computation | async-start | bytes 1048576 | tf_op jit(solution)/shard_map/while/body/eval_jaxpr/all_to_all | solution.py:36
  503.8 16.1 %all-to-all-start.1 = ((bf16[32,2,4096]{2,1,0:T(2,128)(2,1)}), bf16[32,2,4096]{2,1,0:T(2,128)(2,1)S(1)}, u32[]{:S(2)}, u32[]{:S(2)}) async-start(bf16[32,2,4096]{2,1,0:T(2,128)(2,1)} %reshape.303), calls=%async_computation.1 | async-start | bytes 1048576 | tf_op jit(solution)/shard_map/while/body/eval_jaxpr/all_to_all | solution.py:51
  521.8 15.7 %all-to-all-start.2 = ((bf16[32,2,4096]{2,1,0:T(2,128)(2,1)}), bf16[32,2,4096]{2,1,0:T(2,128)(2,1)}, u32[]{:S(2)}, u32[]{:S(2)}) async-start(bf16[32,2,4096]{2,1,0:T(2,128)(2,1)} %broadcast_in_dim.183), calls=%async_computation.2 | async-start | bytes 1048576 | tf_op jit(solution)/shard_map/while/body/eval_jaxpr/all_to_all | solution.py:36
  545.9 15.2 %all-to-all-start.3 = ((bf16[32,2,4096]{2,1,0:T(2,128)(2,1)}), bf16[32,2,4096]{2,1,0:T(2,128)(2,1)S(1)}, u32[]{:S(2)}, u32[]{:S(2)}) async-start(bf16[32,2,4096]{2,1,0:T(2,128)(2,1)} %reshape.305), calls=%async_computation.3 | async-start | bytes 1048576 | tf_op jit(solution)/shard_map/while/body/eval_jaxpr/all_to_all | solution.py:51
  549.6 12.0 %collective-permute-start.1 = (bf16[1,2,4096]{2,1,0:T(2,128)(2,1)S(1)}, bf16[1,2,4096]{2,1,0:T(2,128)(2,1)S(1)}, u32[]{:S(2)}, u32[]{:S(2)}) collective-permute-start(bf16[1,2,4096]{2,1,0:T(2,128)(2,1)S(1)} %broadcast_select_fusion.5), channel_id=1, source_target_pairs={{0,96},{32,0},{64,32},{96,64},{1,97},{33,1},{65,33},{97,65},{2,98}... | collective-permute-start | bytes 49160 | tf_op jit(solution)/shard_map/while/body/eval_jaxpr/ppermute | solution.py:57
  561.5 3.9 collective-permute-start
  566.9 16.4 %all-to-all-start = ((bf16[32,2,4096]{2,1,0:T(2,128)(2,1)}), bf16[32,2,4096]{2,1,0:T(2,128)(2,1)S(1)}, u32[]{:S(2)}, u32[]{:S(2)}) async-start(bf16[32,2,4096]{2,1,0:T(2,128)(2,1)} %broadcast_in_dim.182), calls=%async_computation | async-start | bytes 1048576 | tf_op jit(solution)/shard_map/while/body/eval_jaxpr/all_to_all | solution.py:36
  612.9 16.1 %all-to-all-start.1 = ((bf16[32,2,4096]{2,1,0:T(2,128)(2,1)}), bf16[32,2,4096]{2,1,0:T(2,128)(2,1)S(1)}, u32[]{:S(2)}, u32[]{:S(2)}) async-start(bf16[32,2,4096]{2,1,0:T(2,128)(2,1)} %reshape.303), calls=%async_computation.1 | async-start | bytes 1048576 | tf_op jit(solution)/shard_map/while/body/eval_jaxpr/all_to_all | solution.py:51
  630.9 15.7 %all-to-all-start.2 = ((bf16[32,2,4096]{2,1,0:T(2,128)(2,1)}), bf16[32,2,4096]{2,1,0:T(2,128)(2,1)}, u32[]{:S(2)}, u32[]{:S(2)}) async-start(bf16[32,2,4096]{2,1,0:T(2,128)(2,1)} %broadcast_in_dim.183), calls=%async_computation.2 | async-start | bytes 1048576 | tf_op jit(solution)/shard_map/while/body/eval_jaxpr/all_to_all | solution.py:36
  655.0 15.2 %all-to-all-start.3 = ((bf16[32,2,4096]{2,1,0:T(2,128)(2,1)}), bf16[32,2,4096]{2,1,0:T(2,128)(2,1)S(1)}, u32[]{:S(2)}, u32[]{:S(2)}) async-start(bf16[32,2,4096]{2,1,0:T(2,128)(2,1)} %reshape.305), calls=%async_computation.3 | async-start | bytes 1048576 | tf_op jit(solution)/shard_map/while/body/eval_jaxpr/all_to_all | solution.py:51
  658.7 12.0 %collective-permute-start.1 = (bf16[1,2,4096]{2,1,0:T(2,128)(2,1)S(1)}, bf16[1,2,4096]{2,1,0:T(2,128)(2,1)S(1)}, u32[]{:S(2)}, u32[]{:S(2)}) collective-permute-start(bf16[1,2,4096]{2,1,0:T(2,128)(2,1)S(1)} %broadcast_select_fusion.5), channel_id=1, source_target_pairs={{0,96},{32,0},{64,32},{96,64},{1,97},{33,1},{65,33},{97,65},{2,98}... | collective-permute-start | bytes 49160 | tf_op jit(solution)/shard_map/while/body/eval_jaxpr/ppermute | solution.py:57
  670.6 3.9 collective-permute-start
  676.0 16.4 %all-to-all-start = ((bf16[32,2,4096]{2,1,0:T(2,128)(2,1)}), bf16[32,2,4096]{2,1,0:T(2,128)(2,1)S(1)}, u32[]{:S(2)}, u32[]{:S(2)}) async-start(bf16[32,2,4096]{2,1,0:T(2,128)(2,1)} %broadcast_in_dim.182), calls=%async_computation | async-start | bytes 1048576 | tf_op jit(solution)/shard_map/while/body/eval_jaxpr/all_to_all | solution.py:36
  722.0 16.1 %all-to-all-start.1 = ((bf16[32,2,4096]{2,1,0:T(2,128)(2,1)}), bf16[32,2,4096]{2,1,0:T(2,128)(2,1)S(1)}, u32[]{:S(2)}, u32[]{:S(2)}) async-start(bf16[32,2,4096]{2,1,0:T(2,128)(2,1)} %reshape.303), calls=%async_computation.1 | async-start | bytes 1048576 | tf_op jit(solution)/shard_map/while/body/eval_jaxpr/all_to_all | solution.py:51
  740.0 15.7 %all-to-all-start.2 = ((bf16[32,2,4096]{2,1,0:T(2,128)(2,1)}), bf16[32,2,4096]{2,1,0:T(2,128)(2,1)}, u32[]{:S(2)}, u32[]{:S(2)}) async-start(bf16[32,2,4096]{2,1,0:T(2,128)(2,1)} %broadcast_in_dim.183), calls=%async_computation.2 | async-start | bytes 1048576 | tf_op jit(solution)/shard_map/while/body/eval_jaxpr/all_to_all | solution.py:36
  764.1 15.2 %all-to-all-start.3 = ((bf16[32,2,4096]{2,1,0:T(2,128)(2,1)}), bf16[32,2,4096]{2,1,0:T(2,128)(2,1)S(1)}, u32[]{:S(2)}, u32[]{:S(2)}) async-start(bf16[32,2,4096]{2,1,0:T(2,128)(2,1)} %reshape.305), calls=%async_computation.3 | async-start | bytes 1048576 | tf_op jit(solution)/shard_map/while/body/eval_jaxpr/all_to_all | solution.py:51
  767.8 12.0 %collective-permute-start.1 = (bf16[1,2,4096]{2,1,0:T(2,128)(2,1)S(1)}, bf16[1,2,4096]{2,1,0:T(2,128)(2,1)S(1)}, u32[]{:S(2)}, u32[]{:S(2)}) collective-permute-start(bf16[1,2,4096]{2,1,0:T(2,128)(2,1)S(1)} %broadcast_select_fusion.5), channel_id=1, source_target_pairs={{0,96},{32,0},{64,32},{96,64},{1,97},{33,1},{65,33},{97,65},{2,98}... | collective-permute-start | bytes 49160 | tf_op jit(solution)/shard_map/while/body/eval_jaxpr/ppermute | solution.py:57
  779.7 3.9 collective-permute-start
  785.1 16.4 %all-to-all-start = ((bf16[32,2,4096]{2,1,0:T(2,128)(2,1)}), bf16[32,2,4096]{2,1,0:T(2,128)(2,1)S(1)}, u32[]{:S(2)}, u32[]{:S(2)}) async-start(bf16[32,2,4096]{2,1,0:T(2,128)(2,1)} %broadcast_in_dim.182), calls=%async_computation | async-start | bytes 1048576 | tf_op jit(solution)/shard_map/while/body/eval_jaxpr/all_to_all | solution.py:36
  831.1 16.1 %all-to-all-start.1 = ((bf16[32,2,4096]{2,1,0:T(2,128)(2,1)}), bf16[32,2,4096]{2,1,0:T(2,128)(2,1)S(1)}, u32[]{:S(2)}, u32[]{:S(2)}) async-start(bf16[32,2,4096]{2,1,0:T(2,128)(2,1)} %reshape.303), calls=%async_computation.1 | async-start | bytes 1048576 | tf_op jit(solution)/shard_map/while/body/eval_jaxpr/all_to_all | solution.py:51
  849.1 15.7 %all-to-all-start.2 = ((bf16[32,2,4096]{2,1,0:T(2,128)(2,1)}), bf16[32,2,4096]{2,1,0:T(2,128)(2,1)}, u32[]{:S(2)}, u32[]{:S(2)}) async-start(bf16[32,2,4096]{2,1,0:T(2,128)(2,1)} %broadcast_in_dim.183), calls=%async_computation.2 | async-start | bytes 1048576 | tf_op jit(solution)/shard_map/while/body/eval_jaxpr/all_to_all | solution.py:36
  873.2 15.2 %all-to-all-start.3 = ((bf16[32,2,4096]{2,1,0:T(2,128)(2,1)}), bf16[32,2,4096]{2,1,0:T(2,128)(2,1)S(1)}, u32[]{:S(2)}, u32[]{:S(2)}) async-start(bf16[32,2,4096]{2,1,0:T(2,128)(2,1)} %reshape.305), calls=%async_computation.3 | async-start | bytes 1048576 | tf_op jit(solution)/shard_map/while/body/eval_jaxpr/all_to_all | solution.py:51
  876.9 12.0 %collective-permute-start.1 = (bf16[1,2,4096]{2,1,0:T(2,128)(2,1)S(1)}, bf16[1,2,4096]{2,1,0:T(2,128)(2,1)S(1)}, u32[]{:S(2)}, u32[]{:S(2)}) collective-permute-start(bf16[1,2,4096]{2,1,0:T(2,128)(2,1)S(1)} %broadcast_select_fusion.5), channel_id=1, source_target_pairs={{0,96},{32,0},{64,32},{96,64},{1,97},{33,1},{65,33},{97,65},{2,98}... | collective-permute-start | bytes 49160 | tf_op jit(solution)/shard_map/while/body/eval_jaxpr/ppermute | solution.py:57
  888.8 3.9 collective-permute-start
  (13 other events, 56.0 us)
where the time goes:
time: 915 us; the launch traced here: 910 us
  waiting for transfers between devices  371 us (41%)
  blocking collectives  200 us (22%)
  starting transfers between devices  150 us (16%)
  matrix products  74.9 us (8%)
  local copies, waits for them, and re-layouts  73 us (8%)
  other arithmetic  34.3 us (4%)
    all_gather x8, blocking collectives, rows_first(): out = lax.all_gather(both, axis, axis=0, tiled=True)  184 us
    all_to_all x16, waiting for transfers between devices, summed_on_arrival(): lax.all_to_all(in_blocks(array, dim, peers), axis, 0, 0, tiled=True)  179 us
    all_to_all x16, waiting for transfers between devices, sent_to_all(): return lax.all_to_all(copies, axis, split_axis=0, concat_axis=0, tiled=True)  163 us
    all_to_all x16, starting transfers between devices, sent_to_all(): return lax.all_to_all(copies, axis, split_axis=0, concat_axis=0, tiled=True)  77.6 us
    all_to_all x16, starting transfers between devices, summed_on_arrival(): lax.all_to_all(in_blocks(array, dim, peers), axis, 0, 0, tiled=True)  65.5 us
    dot_general x8, matrix products, layer_rows(): jnp.dot(collect(normed_ffn, 'mp', 0), joined_pair[layer_pos], preferred_e...  40.8 us
    ppermute x16, waiting for transfers between devices, passed_along(): lax.ppermute(array, axis, [(i, (i + by) % peers) for i in range(peers)])  29.3 us
    broadcast_in_dim x17, local copies, waits for them, and re-layouts, sent_to_all(): copies = jnp.broadcast_to(array, (lax.axis_size(axis), *array.shape))  20.8 us
  transfers between devices with their start and end apart: 48, of which 40 were waited for; matrix products, arithmetic and copies ran while one was open for 2% of the time, Pallas kernels for 0%

commit v1 on v0

--- a/solution.py
+++ b/solution.py
@@ -15,7 +15,9 @@
     turned = [jnp.moveaxis(a, dim, 0) for a, dim in zip(arrays, dims)]
     widths = [t[0].size for t in turned]
     both = jnp.concatenate([t.reshape(-1, w) for t, w in zip(turned, widths)], axis=1)
-    out = lax.all_gather(both, axis, axis=0, tiled=True)
+    out = jnp.concatenate(
+        lax.all_to_all(jnp.stack([both] * lax.axis_size(axis)), axis, 0, 0), axis=0
+    )
     pieces = jnp.split(out, [sum(widths[:k]) for k in range(1, len(widths))], axis=1)
     return tuple(
         (

time: 915 us -> 825 us (0.902)
  blocking collectives: 200 us -> 150 us
  waiting for transfers between devices: 371 us -> 350 us
  starting transfers between devices: 150 us -> 131 us
    all_gather x8 -> x0, blocking collectives: 184 us -> none  [rows_first(): out = lax.all_gather(both, axis, axis=0, tiled=True)]
    all_to_all x1 -> x9, blocking collectives: 16.2 us -> 150 us  [sent_to_all(): return lax.all_to_all(copies, axis, split_axis=0, concat_axis=0, tiled=True)]
    all_to_all x16 -> x8, waiting for transfers between devices: 163 us -> 80 us  [sent_to_all(): return lax.all_to_all(copies, axis, split_axis=0, concat_axis=0, tiled=True)]
    all_to_all x0 -> x8, waiting for transfers between devices: none -> 61.2 us  [rows_first(): lax.all_to_all(jnp.stack([both] * lax.axis_size(axis)), axis, 0, 0)]
    all_to_all x16 -> x8, starting transfers between devices: 77.6 us -> 35.2 us  [sent_to_all(): return lax.all_to_all(copies, axis, split_axis=0, concat_axis=0, tiled=True)]
    all_to_all x0 -> x8, starting transfers between devices: none -> 29.3 us  [rows_first(): lax.all_to_all(jnp.stack([both] * lax.axis_size(axis)), axis, 0, 0)]
where the time goes in v1:
time: 825 us; the launch traced here: 820 us
  waiting for transfers between devices  350 us (42%)
  blocking collectives  150 us (18%)
  starting transfers between devices  131 us (16%)
  matrix products  74.9 us (9%)
  local copies, waits for them, and re-layouts  72.6 us (9%)
  other arithmetic  34.4 us (4%)
    all_to_all x16, waiting for transfers between devices, summed_on_arrival(): lax.all_to_all(in_blocks(array, dim, peers), axis, 0, 0, tiled=True)  180 us
    all_to_all x9, blocking collectives, sent_to_all(): return lax.all_to_all(copies, axis, split_axis=0, concat_axis=0, tiled=True)  150 us
    all_to_all x8, waiting for transfers between devices, sent_to_all(): return lax.all_to_all(copies, axis, split_axis=0, concat_axis=0, tiled=True)  80 us
    all_to_all x8, waiting for transfers between devices, rows_first(): lax.all_to_all(jnp.stack([both] * lax.axis_size(axis)), axis, 0, 0)  61.2 us
    all_to_all x16, starting transfers between devices, summed_on_arrival(): lax.all_to_all(in_blocks(array, dim, peers), axis, 0, 0, tiled=True)  59.3 us
    dot_general x8, matrix products, layer_rows(): jnp.dot(collect(normed_ffn, 'mp', 0), joined_pair[layer_pos], preferred_e...  40.8 us
    all_to_all x8, starting transfers between devices, sent_to_all(): return lax.all_to_all(copies, axis, split_axis=0, concat_axis=0, tiled=True)  35.2 us
    ppermute x16, waiting for transfers between devices, passed_along(): lax.ppermute(array, axis, [(i, (i + by) % peers) for i in range(peers)])  29.3 us
  transfers between devices with their start and end apart: 48, of which 40 were waited for; matrix products, arithmetic and copies ran while one was open for 2% of the time, Pallas kernels for 0%

profile of v1, /device:TPU:1, one launch (start us, length us, event | category | flops | bytes accessed | tf_op | source)
XLA Modules:
  0.0 820.0 jit_solution(14281305434111085855)
XLA Ops:
  4.7 7.9 pad_maximum_fusion.1
  15.2 787.2 %while.21 = (s32[]{:T(128)}, bf16[2,4096]{1,0:T(2,128)(2,1)S(1)}, bf16[1,2,4096]{2,1,0:T(2,128)(2,1)S(1)}, pred[]{:T(512)}, s32[]{:T(128)}, /*index=5*/s32[]{:T(...) while((s32[]{:T(128)}, bf16[2,4096]{1,0:T(2,128)(2,1)S(1)}, ...), condition=%wide.region_7.8_spmd, body=%wide.region_0.7_spmd.sunk | while | flops 977384448 | bytes 49401160 | solution.py:215
  16.0 20.8 %all_to_all.71 = bf16[32,2,4096]{2,1,0:T(2,128)(2,1)S(1)} all-to-all(bf16[32,2,4096]{2,1,0:T(2,128)(2,1)S(1)} %broadcast_in_dim.182), channel_id=1, replica_groups=mesh['section'=4,'mp'=32] {'mp'}, dimensions={0} | all-to-all | bytes 1048576 | tf_op jit(solution)/shard_map/while/body/eval_jaxpr/all_to_all | solution.py:38
  45.3 7.6 all-to-all-done.1
  60.5 11.7 %all-to-all-done.2 = bf16[32,2,4096]{2,1,0:T(2,128)(2,1)S(1)} async-done(((bf16[32,2,4096]{2,1,0:T(2,128)(2,1)}), bf16[32,2,4096]{2,1,0:T(2,128)(2,1)S(1)}, u32[]{:S(2)}, u32[]{:S(2)}) %all-to-all-start.2) | async-done | bytes 524320 | tf_op jit(solution)/shard_map/while/body/eval_jaxpr/all_to_all | solution.py:53
  79.8 10.0 %all-to-all-done.3 = bf16[32,2,4096]{2,1,0:T(2,128)(2,1)} async-done(((bf16[32,2,4096]{2,1,0:T(2,128)(2,1)}), bf16[32,2,4096]{2,1,0:T(2,128)(2,1)}, u32[]{:S(2)}, u32[]{:S(2)}) %all-to-all-start.3) | async-done | bytes 524320 | tf_op jit(solution)/shard_map/while/body/eval_jaxpr/all_to_all | solution.py:38
  91.1 5.1 fusion.82
  104.7 8.7 %all-to-all-done.4 = bf16[32,2,4096]{2,1,0:T(2,128)(2,1)S(1)} async-done(((bf16[32,2,4096]{2,1,0:T(2,128)(2,1)}), bf16[32,2,4096]{2,1,0:T(2,128)(2,1)S(1)}, u32[]{:S(2)}, u32[]{:S(2)}) %all-to-all-start.4) | async-done | bytes 524320 | tf_op jit(solution)/shard_map/while/body/eval_jaxpr/all_to_all | solution.py:53
  118.8 15.7 %all_to_all.71 = bf16[32,2,4096]{2,1,0:T(2,128)(2,1)S(1)} all-to-all(bf16[32,2,4096]{2,1,0:T(2,128)(2,1)S(1)} %broadcast_in_dim.182), channel_id=1, replica_groups=mesh['section'=4,'mp'=32] {'mp'}, dimensions={0} | all-to-all | bytes 1048576 | tf_op jit(solution)/shard_map/while/body/eval_jaxpr/all_to_all | solution.py:38
  143.1 7.6 all-to-all-done.1
  158.3 11.7 %all-to-all-done.2 = bf16[32,2,4096]{2,1,0:T(2,128)(2,1)S(1)} async-done(((bf16[32,2,4096]{2,1,0:T(2,128)(2,1)}), bf16[32,2,4096]{2,1,0:T(2,128)(2,1)S(1)}, u32[]{:S(2)}, u32[]{:S(2)}) %all-to-all-start.2) | async-done | bytes 524320 | tf_op jit(solution)/shard_map/while/body/eval_jaxpr/all_to_all | solution.py:53
  177.6 10.0 %all-to-all-done.3 = bf16[32,2,4096]{2,1,0:T(2,128)(2,1)} async-done(((bf16[32,2,4096]{2,1,0:T(2,128)(2,1)}), bf16[32,2,4096]{2,1,0:T(2,128)(2,1)}, u32[]{:S(2)}, u32[]{:S(2)}) %all-to-all-start.3) | async-done | bytes 524320 | tf_op jit(solution)/shard_map/while/body/eval_jaxpr/all_to_all | solution.py:38
  188.9 5.1 fusion.82
  201.3 9.9 %all-to-all-done.4 = bf16[32,2,4096]{2,1,0:T(2,128)(2,1)S(1)} async-done(((bf16[32,2,4096]{2,1,0:T(2,128)(2,1)}), bf16[32,2,4096]{2,1,0:T(2,128)(2,1)S(1)}, u32[]{:S(2)}, u32[]{:S(2)}) %all-to-all-start.4) | async-done | bytes 524320 | tf_op jit(solution)/shard_map/while/body/eval_jaxpr/all_to_all | solution.py:53
  216.2 16.2 %all_to_all.71 = bf16[32,2,4096]{2,1,0:T(2,128)(2,1)S(1)} all-to-all(bf16[32,2,4096]{2,1,0:T(2,128)(2,1)S(1)} %broadcast_in_dim.182), channel_id=1, replica_groups=mesh['section'=4,'mp'=32] {'mp'}, dimensions={0} | all-to-all | bytes 1048576 | tf_op jit(solution)/shard_map/while/body/eval_jaxpr/all_to_all | solution.py:38
  240.9 7.7 all-to-all-done.1
  256.1 11.7 %all-to-all-done.2 = bf16[32,2,4096]{2,1,0:T(2,128)(2,1)S(1)} async-done(((bf16[32,2,4096]{2,1,0:T(2,128)(2,1)}), bf16[32,2,4096]{2,1,0:T(2,128)(2,1)S(1)}, u32[]{:S(2)}, u32[]{:S(2)}) %all-to-all-start.2) | async-done | bytes 524320 | tf_op jit(solution)/shard_map/while/body/eval_jaxpr/all_to_all | solution.py:53
  275.4 10.0 %all-to-all-done.3 = bf16[32,2,4096]{2,1,0:T(2,128)(2,1)} async-done(((bf16[32,2,4096]{2,1,0:T(2,128)(2,1)}), bf16[32,2,4096]{2,1,0:T(2,128)(2,1)}, u32[]{:S(2)}, u32[]{:S(2)}) %all-to-all-start.3) | async-done | bytes 524320 | tf_op jit(solution)/shard_map/while/body/eval_jaxpr/all_to_all | solution.py:38
  286.7 5.1 fusion.82
  297.9 11.1 %all-to-all-done.4 = bf16[32,2,4096]{2,1,0:T(2,128)(2,1)S(1)} async-done(((bf16[32,2,4096]{2,1,0:T(2,128)(2,1)}), bf16[32,2,4096]{2,1,0:T(2,128)(2,1)S(1)}, u32[]{:S(2)}, u32[]{:S(2)}) %all-to-all-start.4) | async-done | bytes 524320 | tf_op jit(solution)/shard_map/while/body/eval_jaxpr/all_to_all | solution.py:53
  314.1 16.2 %all_to_all.71 = bf16[32,2,4096]{2,1,0:T(2,128)(2,1)S(1)} all-to-all(bf16[32,2,4096]{2,1,0:T(2,128)(2,1)S(1)} %broadcast_in_dim.182), channel_id=1, replica_groups=mesh['section'=4,'mp'=32] {'mp'}, dimensions={0} | all-to-all | bytes 1048576 | tf_op jit(solution)/shard_map/while/body/eval_jaxpr/all_to_all | solution.py:38
  338.8 7.6 all-to-all-done.1
  354.0 11.7 %all-to-all-done.2 = bf16[32,2,4096]{2,1,0:T(2,128)(2,1)S(1)} async-done(((bf16[32,2,4096]{2,1,0:T(2,128)(2,1)}), bf16[32,2,4096]{2,1,0:T(2,128)(2,1)S(1)}, u32[]{:S(2)}, u32[]{:S(2)}) %all-to-all-start.2) | async-done | bytes 524320 | tf_op jit(solution)/shard_map/while/body/eval_jaxpr/all_to_all | solution.py:53
  373.3 10.0 %all-to-all-done.3 = bf16[32,2,4096]{2,1,0:T(2,128)(2,1)} async-done(((bf16[32,2,4096]{2,1,0:T(2,128)(2,1)}), bf16[32,2,4096]{2,1,0:T(2,128)(2,1)}, u32[]{:S(2)}, u32[]{:S(2)}) %all-to-all-start.3) | async-done | bytes 524320 | tf_op jit(solution)/shard_map/while/body/eval_jaxpr/all_to_all | solution.py:38
  384.5 5.1 fusion.82
  395.4 11.4 %all-to-all-done.4 = bf16[32,2,4096]{2,1,0:T(2,128)(2,1)S(1)} async-done(((bf16[32,2,4096]{2,1,0:T(2,128)(2,1)}), bf16[32,2,4096]{2,1,0:T(2,128)(2,1)S(1)}, u32[]{:S(2)}, u32[]{:S(2)}) %all-to-all-start.4) | async-done | bytes 524320 | tf_op jit(solution)/shard_map/while/body/eval_jaxpr/all_to_all | solution.py:53
  411.9 16.2 %all_to_all.71 = bf16[32,2,4096]{2,1,0:T(2,128)(2,1)S(1)} all-to-all(bf16[32,2,4096]{2,1,0:T(2,128)(2,1)S(1)} %broadcast_in_dim.182), channel_id=1, replica_groups=mesh['section'=4,'mp'=32] {'mp'}, dimensions={0} | all-to-all | bytes 1048576 | tf_op jit(solution)/shard_map/while/body/eval_jaxpr/all_to_all | solution.py:38
  436.6 7.7 all-to-all-done.1
  451.8 11.7 %all-to-all-done.2 = bf16[32,2,4096]{2,1,0:T(2,128)(2,1)S(1)} async-done(((bf16[32,2,4096]{2,1,0:T(2,128)(2,1)}), bf16[32,2,4096]{2,1,0:T(2,128)(2,1)S(1)}, u32[]{:S(2)}, u32[]{:S(2)}) %all-to-all-start.2) | async-done | bytes 524320 | tf_op jit(solution)/shard_map/while/body/eval_jaxpr/all_to_all | solution.py:53
  471.1 10.0 %all-to-all-done.3 = bf16[32,2,4096]{2,1,0:T(2,128)(2,1)} async-done(((bf16[32,2,4096]{2,1,0:T(2,128)(2,1)}), bf16[32,2,4096]{2,1,0:T(2,128)(2,1)}, u32[]{:S(2)}, u32[]{:S(2)}) %all-to-all-start.3) | async-done | bytes 524320 | tf_op jit(solution)/shard_map/while/body/eval_jaxpr/all_to_all | solution.py:38
  482.3 5.1 fusion.82
  493.2 11.4 %all-to-all-done.4 = bf16[32,2,4096]{2,1,0:T(2,128)(2,1)S(1)} async-done(((bf16[32,2,4096]{2,1,0:T(2,128)(2,1)}), bf16[32,2,4096]{2,1,0:T(2,128)(2,1)S(1)}, u32[]{:S(2)}, u32[]{:S(2)}) %all-to-all-start.4) | async-done | bytes 524320 | tf_op jit(solution)/shard_map/while/body/eval_jaxpr/all_to_all | solution.py:53
  509.7 16.2 %all_to_all.71 = bf16[32,2,4096]{2,1,0:T(2,128)(2,1)S(1)} all-to-all(bf16[32,2,4096]{2,1,0:T(2,128)(2,1)S(1)} %broadcast_in_dim.182), channel_id=1, replica_groups=mesh['section'=4,'mp'=32] {'mp'}, dimensions={0} | all-to-all | bytes 1048576 | tf_op jit(solution)/shard_map/while/body/eval_jaxpr/all_to_all | solution.py:38
  534.4 7.6 all-to-all-done.1
  549.6 11.7 %all-to-all-done.2 = bf16[32,2,4096]{2,1,0:T(2,128)(2,1)S(1)} async-done(((bf16[32,2,4096]{2,1,0:T(2,128)(2,1)}), bf16[32,2,4096]{2,1,0:T(2,128)(2,1)S(1)}, u32[]{:S(2)}, u32[]{:S(2)}) %all-to-all-start.2) | async-done | bytes 524320 | tf_op jit(solution)/shard_map/while/body/eval_jaxpr/all_to_all | solution.py:53
  568.9 10.0 %all-to-all-done.3 = bf16[32,2,4096]{2,1,0:T(2,128)(2,1)} async-done(((bf16[32,2,4096]{2,1,0:T(2,128)(2,1)}), bf16[32,2,4096]{2,1,0:T(2,128)(2,1)}, u32[]{:S(2)}, u32[]{:S(2)}) %all-to-all-start.3) | async-done | bytes 524320 | tf_op jit(solution)/shard_map/while/body/eval_jaxpr/all_to_all | solution.py:38
  591.0 11.4 %all-to-all-done.4 = bf16[32,2,4096]{2,1,0:T(2,128)(2,1)S(1)} async-done(((bf16[32,2,4096]{2,1,0:T(2,128)(2,1)}), bf16[32,2,4096]{2,1,0:T(2,128)(2,1)S(1)}, u32[]{:S(2)}, u32[]{:S(2)}) %all-to-all-start.4) | async-done | bytes 524320 | tf_op jit(solution)/shard_map/while/body/eval_jaxpr/all_to_all | solution.py:53
  607.5 16.2 %all_to_all.71 = bf16[32,2,4096]{2,1,0:T(2,128)(2,1)S(1)} all-to-all(bf16[32,2,4096]{2,1,0:T(2,128)(2,1)S(1)} %broadcast_in_dim.182), channel_id=1, replica_groups=mesh['section'=4,'mp'=32] {'mp'}, dimensions={0} | all-to-all | bytes 1048576 | tf_op jit(solution)/shard_map/while/body/eval_jaxpr/all_to_all | solution.py:38
  632.2 7.7 all-to-all-done.1
  647.4 11.7 %all-to-all-done.2 = bf16[32,2,4096]{2,1,0:T(2,128)(2,1)S(1)} async-done(((bf16[32,2,4096]{2,1,0:T(2,128)(2,1)}), bf16[32,2,4096]{2,1,0:T(2,128)(2,1)S(1)}, u32[]{:S(2)}, u32[]{:S(2)}) %all-to-all-start.2) | async-done | bytes 524320 | tf_op jit(solution)/shard_map/while/body/eval_jaxpr/all_to_all | solution.py:53
  666.7 10.0 %all-to-all-done.3 = bf16[32,2,4096]{2,1,0:T(2,128)(2,1)} async-done(((bf16[32,2,4096]{2,1,0:T(2,128)(2,1)}), bf16[32,2,4096]{2,1,0:T(2,128)(2,1)}, u32[]{:S(2)}, u32[]{:S(2)}) %all-to-all-start.3) | async-done | bytes 524320 | tf_op jit(solution)/shard_map/while/body/eval_jaxpr/all_to_all | solution.py:38
  688.9 11.4 %all-to-all-done.4 = bf16[32,2,4096]{2,1,0:T(2,128)(2,1)S(1)} async-done(((bf16[32,2,4096]{2,1,0:T(2,128)(2,1)}), bf16[32,2,4096]{2,1,0:T(2,128)(2,1)S(1)}, u32[]{:S(2)}, u32[]{:S(2)}) %all-to-all-start.4) | async-done | bytes 524320 | tf_op jit(solution)/shard_map/while/body/eval_jaxpr/all_to_all | solution.py:53
  705.3 16.2 %all_to_all.71 = bf16[32,2,4096]{2,1,0:T(2,128)(2,1)S(1)} all-to-all(bf16[32,2,4096]{2,1,0:T(2,128)(2,1)S(1)} %broadcast_in_dim.182), channel_id=1, replica_groups=mesh['section'=4,'mp'=32] {'mp'}, dimensions={0} | all-to-all | bytes 1048576 | tf_op jit(solution)/shard_map/while/body/eval_jaxpr/all_to_all | solution.py:38
  730.0 7.6 all-to-all-done.1
  745.2 11.7 %all-to-all-done.2 = bf16[32,2,4096]{2,1,0:T(2,128)(2,1)S(1)} async-done(((bf16[32,2,4096]{2,1,0:T(2,128)(2,1)}), bf16[32,2,4096]{2,1,0:T(2,128)(2,1)S(1)}, u32[]{:S(2)}, u32[]{:S(2)}) %all-to-all-start.2) | async-done | bytes 524320 | tf_op jit(solution)/shard_map/while/body/eval_jaxpr/all_to_all | solution.py:53
  764.5 10.0 %all-to-all-done.3 = bf16[32,2,4096]{2,1,0:T(2,128)(2,1)} async-done(((bf16[32,2,4096]{2,1,0:T(2,128)(2,1)}), bf16[32,2,4096]{2,1,0:T(2,128)(2,1)}, u32[]{:S(2)}, u32[]{:S(2)}) %all-to-all-start.3) | async-done | bytes 524320 | tf_op jit(solution)/shard_map/while/body/eval_jaxpr/all_to_all | solution.py:38
  786.7 11.4 %all-to-all-done.4 = bf16[32,2,4096]{2,1,0:T(2,128)(2,1)S(1)} async-done(((bf16[32,2,4096]{2,1,0:T(2,128)(2,1)}), bf16[32,2,4096]{2,1,0:T(2,128)(2,1)S(1)}, u32[]{:S(2)}, u32[]{:S(2)}) %all-to-all-start.4) | async-done | bytes 524320 | tf_op jit(solution)/shard_map/while/body/eval_jaxpr/all_to_all | solution.py:53
  802.9 16.2 %all_to_all.70 = bf16[32,1,2,4096]{3,2,1,0:T(2,128)(2,1)S(1)} all-to-all(bf16[32,1,2,4096]{3,2,1,0:T(2,128)(2,1)S(1)} %broadcast_in_dim.154), channel_id=1, replica_groups=mesh['section'=4,'mp'=32] {'mp'}, dimensions={0} | all-to-all | bytes 1048576 | tf_op jit(solution)/shard_map/all_to_all | solution.py:38
  (404 shorter events, 308.8 us)
Async XLA Ops:
  40.4 12.6 %all-to-all-start.1 = ((bf16[32,32,128]{2,1,0:T(8,128)(2,1)}), bf16[32,32,128]{2,1,0:T(8,128)(2,1)S(1)}, u32[]{:S(2)}, u32[]{:S(2)}) async-start(bf16[32,32,128]{2,1,0:T(8,128)(2,1)} %stack.7), calls=%async_computation.1 | async-start | bytes 524288 | tf_op jit(solution)/shard_map/while/body/eval_jaxpr/all_to_all | solution.py:19
  56.7 15.4 %all-to-all-start.2 = ((bf16[32,2,4096]{2,1,0:T(2,128)(2,1)}), bf16[32,2,4096]{2,1,0:T(2,128)(2,1)S(1)}, u32[]{:S(2)}, u32[]{:S(2)}) async-start(bf16[32,2,4096]{2,1,0:T(2,128)(2,1)} %reshape.315), calls=%async_computation.2 | async-start | bytes 1048576 | tf_op jit(solution)/shard_map/while/body/eval_jaxpr/all_to_all | solution.py:53
  74.1 15.7 %all-to-all-start.3 = ((bf16[32,2,4096]{2,1,0:T(2,128)(2,1)}), bf16[32,2,4096]{2,1,0:T(2,128)(2,1)}, u32[]{:S(2)}, u32[]{:S(2)}) async-start(bf16[32,2,4096]{2,1,0:T(2,128)(2,1)} %broadcast_in_dim.183), calls=%async_computation.3 | async-start | bytes 1048576 | tf_op jit(solution)/shard_map/while/body/eval_jaxpr/all_to_all | solution.py:38
  98.2 15.2 %all-to-all-start.4 = ((bf16[32,2,4096]{2,1,0:T(2,128)(2,1)}), bf16[32,2,4096]{2,1,0:T(2,128)(2,1)S(1)}, u32[]{:S(2)}, u32[]{:S(2)}) async-start(bf16[32,2,4096]{2,1,0:T(2,128)(2,1)} %reshape.317), calls=%async_computation.4 | async-start | bytes 1048576 | tf_op jit(solution)/shard_map/while/body/eval_jaxpr/all_to_all | solution.py:53
  101.9 13.3 %collective-permute-start.1 = (bf16[1,2,4096]{2,1,0:T(2,128)(2,1)S(1)}, bf16[1,2,4096]{2,1,0:T(2,128)(2,1)S(1)}, u32[]{:S(2)}, u32[]{:S(2)}) collective-permute-start(bf16[1,2,4096]{2,1,0:T(2,128)(2,1)S(1)} %broadcast_select_fusion.5), channel_id=1, source_target_pairs={{0,96},{32,0},{64,32},{96,64},{1,97},{33,1},{65,33},{97,65},{2,98}... | collective-permute-start | bytes 49160 | tf_op jit(solution)/shard_map/while/body/eval_jaxpr/ppermute | solution.py:59
  113.8 4.3 collective-permute-start
  138.2 12.6 %all-to-all-start.1 = ((bf16[32,32,128]{2,1,0:T(8,128)(2,1)}), bf16[32,32,128]{2,1,0:T(8,128)(2,1)S(1)}, u32[]{:S(2)}, u32[]{:S(2)}) async-start(bf16[32,32,128]{2,1,0:T(8,128)(2,1)} %stack.7), calls=%async_computation.1 | async-start | bytes 524288 | tf_op jit(solution)/shard_map/while/body/eval_jaxpr/all_to_all | solution.py:19
  154.5 15.4 %all-to-all-start.2 = ((bf16[32,2,4096]{2,1,0:T(2,128)(2,1)}), bf16[32,2,4096]{2,1,0:T(2,128)(2,1)S(1)}, u32[]{:S(2)}, u32[]{:S(2)}) async-start(bf16[32,2,4096]{2,1,0:T(2,128)(2,1)} %reshape.315), calls=%async_computation.2 | async-start | bytes 1048576 | tf_op jit(solution)/shard_map/while/body/eval_jaxpr/all_to_all | solution.py:53
  171.9 15.7 %all-to-all-start.3 = ((bf16[32,2,4096]{2,1,0:T(2,128)(2,1)}), bf16[32,2,4096]{2,1,0:T(2,128)(2,1)}, u32[]{:S(2)}, u32[]{:S(2)}) async-start(bf16[32,2,4096]{2,1,0:T(2,128)(2,1)} %broadcast_in_dim.183), calls=%async_computation.3 | async-start | bytes 1048576 | tf_op jit(solution)/shard_map/while/body/eval_jaxpr/all_to_all | solution.py:38
  196.0 15.2 %all-to-all-start.4 = ((bf16[32,2,4096]{2,1,0:T(2,128)(2,1)}), bf16[32,2,4096]{2,1,0:T(2,128)(2,1)S(1)}, u32[]{:S(2)}, u32[]{:S(2)}) async-start(bf16[32,2,4096]{2,1,0:T(2,128)(2,1)} %reshape.317), calls=%async_computation.4 | async-start | bytes 1048576 | tf_op jit(solution)/shard_map/while/body/eval_jaxpr/all_to_all | solution.py:53
  199.7 12.1 %collective-permute-start.1 = (bf16[1,2,4096]{2,1,0:T(2,128)(2,1)S(1)}, bf16[1,2,4096]{2,1,0:T(2,128)(2,1)S(1)}, u32[]{:S(2)}, u32[]{:S(2)}) collective-permute-start(bf16[1,2,4096]{2,1,0:T(2,128)(2,1)S(1)} %broadcast_select_fusion.5), channel_id=1, source_target_pairs={{0,96},{32,0},{64,32},{96,64},{1,97},{33,1},{65,33},{97,65},{2,98}... | collective-permute-start | bytes 49160 | tf_op jit(solution)/shard_map/while/body/eval_jaxpr/ppermute | solution.py:59
  211.6 3.9 collective-permute-start
  236.0 12.6 %all-to-all-start.1 = ((bf16[32,32,128]{2,1,0:T(8,128)(2,1)}), bf16[32,32,128]{2,1,0:T(8,128)(2,1)S(1)}, u32[]{:S(2)}, u32[]{:S(2)}) async-start(bf16[32,32,128]{2,1,0:T(8,128)(2,1)} %stack.7), calls=%async_computation.1 | async-start | bytes 524288 | tf_op jit(solution)/shard_map/while/body/eval_jaxpr/all_to_all | solution.py:19
  252.4 15.4 %all-to-all-start.2 = ((bf16[32,2,4096]{2,1,0:T(2,128)(2,1)}), bf16[32,2,4096]{2,1,0:T(2,128)(2,1)S(1)}, u32[]{:S(2)}, u32[]{:S(2)}) async-start(bf16[32,2,4096]{2,1,0:T(2,128)(2,1)} %reshape.315), calls=%async_computation.2 | async-start | bytes 1048576 | tf_op jit(solution)/shard_map/while/body/eval_jaxpr/all_to_all | solution.py:53
  269.8 15.7 %all-to-all-start.3 = ((bf16[32,2,4096]{2,1,0:T(2,128)(2,1)}), bf16[32,2,4096]{2,1,0:T(2,128)(2,1)}, u32[]{:S(2)}, u32[]{:S(2)}) async-start(bf16[32,2,4096]{2,1,0:T(2,128)(2,1)} %broadcast_in_dim.183), calls=%async_computation.3 | async-start | bytes 1048576 | tf_op jit(solution)/shard_map/while/body/eval_jaxpr/all_to_all | solution.py:38
  293.8 15.2 %all-to-all-start.4 = ((bf16[32,2,4096]{2,1,0:T(2,128)(2,1)}), bf16[32,2,4096]{2,1,0:T(2,128)(2,1)S(1)}, u32[]{:S(2)}, u32[]{:S(2)}) async-start(bf16[32,2,4096]{2,1,0:T(2,128)(2,1)} %reshape.317), calls=%async_computation.4 | async-start | bytes 1048576 | tf_op jit(solution)/shard_map/while/body/eval_jaxpr/all_to_all | solution.py:53
  297.5 12.0 %collective-permute-start.1 = (bf16[1,2,4096]{2,1,0:T(2,128)(2,1)S(1)}, bf16[1,2,4096]{2,1,0:T(2,128)(2,1)S(1)}, u32[]{:S(2)}, u32[]{:S(2)}) collective-permute-start(bf16[1,2,4096]{2,1,0:T(2,128)(2,1)S(1)} %broadcast_select_fusion.5), channel_id=1, source_target_pairs={{0,96},{32,0},{64,32},{96,64},{1,97},{33,1},{65,33},{97,65},{2,98}... | collective-permute-start | bytes 49160 | tf_op jit(solution)/shard_map/while/body/eval_jaxpr/ppermute | solution.py:59
  309.4 3.9 collective-permute-start
  333.8 12.6 %all-to-all-start.1 = ((bf16[32,32,128]{2,1,0:T(8,128)(2,1)}), bf16[32,32,128]{2,1,0:T(8,128)(2,1)S(1)}, u32[]{:S(2)}, u32[]{:S(2)}) async-start(bf16[32,32,128]{2,1,0:T(8,128)(2,1)} %stack.7), calls=%async_computation.1 | async-start | bytes 524288 | tf_op jit(solution)/shard_map/while/body/eval_jaxpr/all_to_all | solution.py:19
  350.2 15.4 %all-to-all-start.2 = ((bf16[32,2,4096]{2,1,0:T(2,128)(2,1)}), bf16[32,2,4096]{2,1,0:T(2,128)(2,1)S(1)}, u32[]{:S(2)}, u32[]{:S(2)}) async-start(bf16[32,2,4096]{2,1,0:T(2,128)(2,1)} %reshape.315), calls=%async_computation.2 | async-start | bytes 1048576 | tf_op jit(solution)/shard_map/while/body/eval_jaxpr/all_to_all | solution.py:53
  367.6 15.7 %all-to-all-start.3 = ((bf16[32,2,4096]{2,1,0:T(2,128)(2,1)}), bf16[32,2,4096]{2,1,0:T(2,128)(2,1)}, u32[]{:S(2)}, u32[]{:S(2)}) async-start(bf16[32,2,4096]{2,1,0:T(2,128)(2,1)} %broadcast_in_dim.183), calls=%async_computation.3 | async-start | bytes 1048576 | tf_op jit(solution)/shard_map/while/body/eval_jaxpr/all_to_all | solution.py:38
  391.6 15.2 %all-to-all-start.4 = ((bf16[32,2,4096]{2,1,0:T(2,128)(2,1)}), bf16[32,2,4096]{2,1,0:T(2,128)(2,1)S(1)}, u32[]{:S(2)}, u32[]{:S(2)}) async-start(bf16[32,2,4096]{2,1,0:T(2,128)(2,1)} %reshape.317), calls=%async_computation.4 | async-start | bytes 1048576 | tf_op jit(solution)/shard_map/while/body/eval_jaxpr/all_to_all | solution.py:53
  395.3 12.0 %collective-permute-start.1 = (bf16[1,2,4096]{2,1,0:T(2,128)(2,1)S(1)}, bf16[1,2,4096]{2,1,0:T(2,128)(2,1)S(1)}, u32[]{:S(2)}, u32[]{:S(2)}) collective-permute-start(bf16[1,2,4096]{2,1,0:T(2,128)(2,1)S(1)} %broadcast_select_fusion.5), channel_id=1, source_target_pairs={{0,96},{32,0},{64,32},{96,64},{1,97},{33,1},{65,33},{97,65},{2,98}... | collective-permute-start | bytes 49160 | tf_op jit(solution)/shard_map/while/body/eval_jaxpr/ppermute | solution.py:59
  407.3 3.9 collective-permute-start
  431.6 12.6 %all-to-all-start.1 = ((bf16[32,32,128]{2,1,0:T(8,128)(2,1)}), bf16[32,32,128]{2,1,0:T(8,128)(2,1)S(1)}, u32[]{:S(2)}, u32[]{:S(2)}) async-start(bf16[32,32,128]{2,1,0:T(8,128)(2,1)} %stack.7), calls=%async_computation.1 | async-start | bytes 524288 | tf_op jit(solution)/shard_map/while/body/eval_jaxpr/all_to_all | solution.py:19
  448.0 15.4 %all-to-all-start.2 = ((bf16[32,2,4096]{2,1,0:T(2,128)(2,1)}), bf16[32,2,4096]{2,1,0:T(2,128)(2,1)S(1)}, u32[]{:S(2)}, u32[]{:S(2)}) async-start(bf16[32,2,4096]{2,1,0:T(2,128)(2,1)} %reshape.315), calls=%async_computation.2 | async-start | bytes 1048576 | tf_op jit(solution)/shard_map/while/body/eval_jaxpr/all_to_all | solution.py:53
  465.4 15.7 %all-to-all-start.3 = ((bf16[32,2,4096]{2,1,0:T(2,128)(2,1)}), bf16[32,2,4096]{2,1,0:T(2,128)(2,1)}, u32[]{:S(2)}, u32[]{:S(2)}) async-start(bf16[32,2,4096]{2,1,0:T(2,128)(2,1)} %broadcast_in_dim.183), calls=%async_computation.3 | async-start | bytes 1048576 | tf_op jit(solution)/shard_map/while/body/eval_jaxpr/all_to_all | solution.py:38
  489.4 15.2 %all-to-all-start.4 = ((bf16[32,2,4096]{2,1,0:T(2,128)(2,1)}), bf16[32,2,4096]{2,1,0:T(2,128)(2,1)S(1)}, u32[]{:S(2)}, u32[]{:S(2)}) async-start(bf16[32,2,4096]{2,1,0:T(2,128)(2,1)} %reshape.317), calls=%async_computation.4 | async-start | bytes 1048576 | tf_op jit(solution)/shard_map/while/body/eval_jaxpr/all_to_all | solution.py:53
  493.1 12.0 %collective-permute-start.1 = (bf16[1,2,4096]{2,1,0:T(2,128)(2,1)S(1)}, bf16[1,2,4096]{2,1,0:T(2,128)(2,1)S(1)}, u32[]{:S(2)}, u32[]{:S(2)}) collective-permute-start(bf16[1,2,4096]{2,1,0:T(2,128)(2,1)S(1)} %broadcast_select_fusion.5), channel_id=1, source_target_pairs={{0,96},{32,0},{64,32},{96,64},{1,97},{33,1},{65,33},{97,65},{2,98}... | collective-permute-start | bytes 49160 | tf_op jit(solution)/shard_map/while/body/eval_jaxpr/ppermute | solution.py:59
  505.1 3.9 collective-permute-start
  529.5 12.6 %all-to-all-start.1 = ((bf16[32,32,128]{2,1,0:T(8,128)(2,1)}), bf16[32,32,128]{2,1,0:T(8,128)(2,1)S(1)}, u32[]{:S(2)}, u32[]{:S(2)}) async-start(bf16[32,32,128]{2,1,0:T(8,128)(2,1)} %stack.7), calls=%async_computation.1 | async-start | bytes 524288 | tf_op jit(solution)/shard_map/while/body/eval_jaxpr/all_to_all | solution.py:19
  545.8 15.4 %all-to-all-start.2 = ((bf16[32,2,4096]{2,1,0:T(2,128)(2,1)}), bf16[32,2,4096]{2,1,0:T(2,128)(2,1)S(1)}, u32[]{:S(2)}, u32[]{:S(2)}) async-start(bf16[32,2,4096]{2,1,0:T(2,128)(2,1)} %reshape.315), calls=%async_computation.2 | async-start | bytes 1048576 | tf_op jit(solution)/shard_map/while/body/eval_jaxpr/all_to_all | solution.py:53
  563.2 15.7 %all-to-all-start.3 = ((bf16[32,2,4096]{2,1,0:T(2,128)(2,1)}), bf16[32,2,4096]{2,1,0:T(2,128)(2,1)}, u32[]{:S(2)}, u32[]{:S(2)}) async-start(bf16[32,2,4096]{2,1,0:T(2,128)(2,1)} %broadcast_in_dim.183), calls=%async_computation.3 | async-start | bytes 1048576 | tf_op jit(solution)/shard_map/while/body/eval_jaxpr/all_to_all | solution.py:38
  587.2 15.2 %all-to-all-start.4 = ((bf16[32,2,4096]{2,1,0:T(2,128)(2,1)}), bf16[32,2,4096]{2,1,0:T(2,128)(2,1)S(1)}, u32[]{:S(2)}, u32[]{:S(2)}) async-start(bf16[32,2,4096]{2,1,0:T(2,128)(2,1)} %reshape.317), calls=%async_computation.4 | async-start | bytes 1048576 | tf_op jit(solution)/shard_map/while/body/eval_jaxpr/all_to_all | solution.py:53
  591.0 12.0 %collective-permute-start.1 = (bf16[1,2,4096]{2,1,0:T(2,128)(2,1)S(1)}, bf16[1,2,4096]{2,1,0:T(2,128)(2,1)S(1)}, u32[]{:S(2)}, u32[]{:S(2)}) collective-permute-start(bf16[1,2,4096]{2,1,0:T(2,128)(2,1)S(1)} %broadcast_select_fusion.5), channel_id=1, source_target_pairs={{0,96},{32,0},{64,32},{96,64},{1,97},{33,1},{65,33},{97,65},{2,98}... | collective-permute-start | bytes 49160 | tf_op jit(solution)/shard_map/while/body/eval_jaxpr/ppermute | solution.py:59
  602.9 3.9 collective-permute-start
  627.3 12.6 %all-to-all-start.1 = ((bf16[32,32,128]{2,1,0:T(8,128)(2,1)}), bf16[32,32,128]{2,1,0:T(8,128)(2,1)S(1)}, u32[]{:S(2)}, u32[]{:S(2)}) async-start(bf16[32,32,128]{2,1,0:T(8,128)(2,1)} %stack.7), calls=%async_computation.1 | async-start | bytes 524288 | tf_op jit(solution)/shard_map/while/body/eval_jaxpr/all_to_all | solution.py:19
  643.6 15.4 %all-to-all-start.2 = ((bf16[32,2,4096]{2,1,0:T(2,128)(2,1)}), bf16[32,2,4096]{2,1,0:T(2,128)(2,1)S(1)}, u32[]{:S(2)}, u32[]{:S(2)}) async-start(bf16[32,2,4096]{2,1,0:T(2,128)(2,1)} %reshape.315), calls=%async_computation.2 | async-start | bytes 1048576 | tf_op jit(solution)/shard_map/while/body/eval_jaxpr/all_to_all | solution.py:53
  661.0 15.7 %all-to-all-start.3 = ((bf16[32,2,4096]{2,1,0:T(2,128)(2,1)}), bf16[32,2,4096]{2,1,0:T(2,128)(2,1)}, u32[]{:S(2)}, u32[]{:S(2)}) async-start(bf16[32,2,4096]{2,1,0:T(2,128)(2,1)} %broadcast_in_dim.183), calls=%async_computation.3 | async-start | bytes 1048576 | tf_op jit(solution)/shard_map/while/body/eval_jaxpr/all_to_all | solution.py:38
  685.1 15.2 %all-to-all-start.4 = ((bf16[32,2,4096]{2,1,0:T(2,128)(2,1)}), bf16[32,2,4096]{2,1,0:T(2,128)(2,1)S(1)}, u32[]{:S(2)}, u32[]{:S(2)}) async-start(bf16[32,2,4096]{2,1,0:T(2,128)(2,1)} %reshape.317), calls=%async_computation.4 | async-start | bytes 1048576 | tf_op jit(solution)/shard_map/while/body/eval_jaxpr/all_to_all | solution.py:53
  688.8 12.0 %collective-permute-start.1 = (bf16[1,2,4096]{2,1,0:T(2,128)(2,1)S(1)}, bf16[1,2,4096]{2,1,0:T(2,128)(2,1)S(1)}, u32[]{:S(2)}, u32[]{:S(2)}) collective-permute-start(bf16[1,2,4096]{2,1,0:T(2,128)(2,1)S(1)} %broadcast_select_fusion.5), channel_id=1, source_target_pairs={{0,96},{32,0},{64,32},{96,64},{1,97},{33,1},{65,33},{97,65},{2,98}... | collective-permute-start | bytes 49160 | tf_op jit(solution)/shard_map/while/body/eval_jaxpr/ppermute | solution.py:59
  700.7 3.9 collective-permute-start
  725.1 12.6 %all-to-all-start.1 = ((bf16[32,32,128]{2,1,0:T(8,128)(2,1)}), bf16[32,32,128]{2,1,0:T(8,128)(2,1)S(1)}, u32[]{:S(2)}, u32[]{:S(2)}) async-start(bf16[32,32,128]{2,1,0:T(8,128)(2,1)} %stack.7), calls=%async_computation.1 | async-start | bytes 524288 | tf_op jit(solution)/shard_map/while/body/eval_jaxpr/all_to_all | solution.py:19
  741.5 15.4 %all-to-all-start.2 = ((bf16[32,2,4096]{2,1,0:T(2,128)(2,1)}), bf16[32,2,4096]{2,1,0:T(2,128)(2,1)S(1)}, u32[]{:S(2)}, u32[]{:S(2)}) async-start(bf16[32,2,4096]{2,1,0:T(2,128)(2,1)} %reshape.315), calls=%async_computation.2 | async-start | bytes 1048576 | tf_op jit(solution)/shard_map/while/body/eval_jaxpr/all_to_all | solution.py:53
  758.9 15.7 %all-to-all-start.3 = ((bf16[32,2,4096]{2,1,0:T(2,128)(2,1)}), bf16[32,2,4096]{2,1,0:T(2,128)(2,1)}, u32[]{:S(2)}, u32[]{:S(2)}) async-start(bf16[32,2,4096]{2,1,0:T(2,128)(2,1)} %broadcast_in_dim.183), calls=%async_computation.3 | async-start | bytes 1048576 | tf_op jit(solution)/shard_map/while/body/eval_jaxpr/all_to_all | solution.py:38
  782.9 15.2 %all-to-all-start.4 = ((bf16[32,2,4096]{2,1,0:T(2,128)(2,1)}), bf16[32,2,4096]{2,1,0:T(2,128)(2,1)S(1)}, u32[]{:S(2)}, u32[]{:S(2)}) async-start(bf16[32,2,4096]{2,1,0:T(2,128)(2,1)} %reshape.317), calls=%async_computation.4 | async-start | bytes 1048576 | tf_op jit(solution)/shard_map/while/body/eval_jaxpr/all_to_all | solution.py:53
  786.6 12.0 %collective-permute-start.1 = (bf16[1,2,4096]{2,1,0:T(2,128)(2,1)S(1)}, bf16[1,2,4096]{2,1,0:T(2,128)(2,1)S(1)}, u32[]{:S(2)}, u32[]{:S(2)}) collective-permute-start(bf16[1,2,4096]{2,1,0:T(2,128)(2,1)S(1)} %broadcast_select_fusion.5), channel_id=1, source_target_pairs={{0,96},{32,0},{64,32},{96,64},{1,97},{33,1},{65,33},{97,65},{2,98}... | collective-permute-start | bytes 49160 | tf_op jit(solution)/shard_map/while/body/eval_jaxpr/ppermute | solution.py:59
  798.5 3.9 collective-permute-start
  (13 other events, 56.0 us)
